TPU v7x, 32 devices: a whole 2x2x4 slice. The times are simulated.
32 devices in a mesh: seq: 8 (over y, x, core), head: 4 (over z).
Axes of the slice: x: 2, y: 2, z: 4, core: 2. Of those that a mesh axis runs over, the one named last changes fastest.
Arguments:
- query_rows: bfloat16 [1024, 2048], P('seq', 'head'), may hold values from -6 to 6
- key_rows: bfloat16 [1024, 128], P('seq'), may hold values from -6 to 6
- value_rows: bfloat16 [1024, 128], P('seq'), may hold values from -6 to 6
- out_grad: bfloat16 [1024, 2048], P('seq', 'head'), may hold values from -3 to 3
Outputs:
- attended: bfloat16 [1024, 2048], P('seq', 'head')
- query_grad: bfloat16 [1024, 2048], P('seq', 'head')
- key_grad: bfloat16 [1024, 128], P('seq')
- value_grad: bfloat16 [1024, 128], P('seq')
All inputs are finite; a program needn't handle non-finite values.
Results may differ from a plain program's by a relative error of at most 0.023.
Values may be sent and summed in bfloat16 or wider, within the bound.
No kernel may reach another device: no remote copies, remote signals or barrier semaphores. Data moves between devices by JAX's collectives and lax.ppermute only.
A program may use at most 64 MiB of HBM per device.

v0:
```python
import jax
import jax.numpy as jnp
import numpy as np
from jax import lax
from jax.sharding import PartitionSpec as P

EPSILON = 1e-06


def prefix_2(shard, axis, combine, identity):
    length, here = (lax.axis_size(axis), lax.axis_index(axis))
    everything = lax.all_gather(shard, axis)
    start = jnp.broadcast_to(jnp.asarray(identity, shard.dtype), shard.shape)

    def hop(k, before):
        reached = k < here
        new = combine(before, everything[k])
        return jnp.where(reached, new, before)

    return lax.fori_loop(0, length, hop, start)


def prefix_3(shard, axis, combine, identity):
    length, here = (lax.axis_size(axis), lax.axis_index(axis))
    everything = lax.all_gather(shard.astype(jnp.bfloat16), axis)
    start = jnp.broadcast_to(jnp.asarray(identity, shard.dtype), shard.shape)

    def hop(k, before):
        at = length - 1 - k
        reached = at > here
        new = combine(before, everything[at].astype(shard.dtype))
        return jnp.where(reached, new, before)

    return lax.fori_loop(0, length, hop, start)


def pair_tables(head_width):
    first_index, second_index = np.triu_indices(head_width)
    return (jnp.asarray(first_index, dtype=jnp.int32), jnp.asarray(second_index, dtype=jnp.int32))


def picker(picked, head_width):
    return (jnp.arange(head_width, dtype=jnp.int32)[:, None] == picked[None, :]).astype(
        jnp.bfloat16
    )


def columns(source, picked):
    return jnp.dot(source, picker(picked, source.shape[-1]), preferred_element_type=jnp.float32)


def multiplicity(first_index, second_index):
    return jnp.where(first_index == second_index, 1.0, 2.0).astype(jnp.float32)


def query_features(source, first_index, second_index):
    expanded = columns(source, first_index) * columns(source, second_index)
    return (expanded * multiplicity(first_index, second_index)).astype(jnp.bfloat16)


def selector(picked, head_width):
    return (picked[:, None] == jnp.arange(head_width, dtype=jnp.int32)[None, :]).astype(
        jnp.bfloat16
    )


def spread_back(coeffs, source, first_index, second_index):
    head_width = source.shape[-1]
    left_terms = (coeffs * columns(source, second_index)).astype(jnp.bfloat16)
    right_terms = (coeffs * columns(source, first_index)).astype(jnp.bfloat16)
    summed = jnp.dot(
        left_terms, selector(first_index, head_width), preferred_element_type=jnp.float32
    )
    return summed + jnp.dot(
        right_terms, selector(second_index, head_width), preferred_element_type=jnp.float32
    )


def contract_rows(left_side, right_side):
    return lax.dot_general(
        left_side, right_side, (((0,), (0,)), ((), ())), preferred_element_type=jnp.float32
    )


def contract_last(left_side, right_side):
    return lax.dot_general(
        left_side, right_side, (((1,), (1,)), ((), ())), preferred_element_type=jnp.float32
    )


def over_blocks(running_sum, shard_piece, block_size, update):

    def inner_step(position, carried):
        sub_block = lax.dynamic_slice_in_dim(shard_piece, position * block_size, block_size)
        return update(carried, sub_block, position * block_size)

    return lax.fori_loop(0, shard_piece.shape[0] // block_size, inner_step, running_sum)


def local(query_rows, key_rows, value_rows, out_grad):
    row_count, head_width = key_rows.shape
    heads_here = query_rows.shape[1] // head_width
    feat_here = head_width * (head_width + 1) // 2 // lax.axis_size("head")
    first_all, second_all = pair_tables(head_width)
    offset = lax.axis_index("head") * feat_here
    first_mine = lax.dynamic_slice_in_dim(first_all, offset, feat_here)
    second_mine = lax.dynamic_slice_in_dim(second_all, offset, feat_here)
    group_rows = heads_here * row_count
    stacked_query = (
        query_rows.reshape(row_count, heads_here, head_width)
        .transpose(1, 0, 2)
        .reshape(group_rows, head_width)
    )
    stacked_grad = (
        out_grad.reshape(row_count, heads_here, head_width)
        .transpose(1, 0, 2)
        .reshape(group_rows, head_width)
    )
    key_features = (columns(key_rows, first_mine) * columns(key_rows, second_mine)).astype(
        jnp.bfloat16
    )
    local_state = contract_rows(key_features, value_rows)
    prefix = prefix_2(local_state, "seq", jnp.add, jnp.zeros_like(local_state)).astype(jnp.bfloat16)
    zero_rows = jnp.zeros((group_rows, head_width), jnp.float32)
    query_heads = stacked_query.reshape(heads_here, row_count, head_width)
    places = jnp.arange(row_count, dtype=jnp.int32)
    causal = places[:, None] >= places[None, :]
    products = jnp.einsum("hrd,sd->hrs", query_heads, key_rows, preferred_element_type=jnp.float32)
    weights = jnp.where(causal, products * products, 0.0).astype(jnp.bfloat16)
    local_part = jnp.einsum(
        "hrs,sd->hrd", weights, value_rows, preferred_element_type=jnp.float32
    ).reshape(group_rows, head_width)
    all_query = lax.all_gather(stacked_query, "head", axis=0, tiled=True)

    def one_group(position):
        picked = lax.dynamic_slice_in_dim(all_query, position * group_rows, group_rows)
        features = query_features(picked, first_mine, second_mine)
        return jnp.dot(features, prefix, preferred_element_type=jnp.float32)

    groups = lax.map(
        one_group, jnp.arange(group_rows * lax.axis_size("head") // group_rows, dtype=jnp.int32)
    )
    remote_part = lax.psum_scatter(
        groups.reshape(group_rows * lax.axis_size("head"), head_width).astype(jnp.bfloat16),
        "head",
        scatter_dimension=0,
        tiled=True,
    ).astype(jnp.float32)
    numerator = local_part + remote_part
    root_mean = jnp.sqrt(jnp.mean(numerator * numerator, axis=-1, keepdims=True) + EPSILON)
    normed = numerator / root_mean
    attended = (
        normed.astype(jnp.bfloat16)
        .reshape(heads_here, row_count, head_width)
        .transpose(1, 0, 2)
        .reshape(row_count, group_rows // row_count * head_width)
    )
    grad_float = stacked_grad.astype(jnp.float32)
    numer_grad = (
        (grad_float - normed * jnp.mean(grad_float * normed, axis=-1, keepdims=True)) / root_mean
    ).astype(jnp.bfloat16)
    grad_heads = numer_grad.reshape(heads_here, row_count, head_width)
    value_dots = jnp.einsum(
        "hrd,sd->hrs", grad_heads, value_rows, preferred_element_type=jnp.float32
    )
    coefficient = jnp.where(causal, 2.0 * products * value_dots, 0.0).astype(jnp.bfloat16)
    query_local = jnp.einsum(
        "hrs,sd->hrd", coefficient, key_rows, preferred_element_type=jnp.float32
    ).reshape(group_rows, head_width)
    key_local = jnp.einsum(
        "hrs,hrd->sd", coefficient, query_heads, preferred_element_type=jnp.float32
    )
    value_local = jnp.einsum("hrs,hrd->sd", weights, grad_heads, preferred_element_type=jnp.float32)

    def add_query_grad(summed, sub_block, start_feature):
        first_index = lax.dynamic_slice_in_dim(first_all, start_feature, sub_block.shape[0])
        second_index = lax.dynamic_slice_in_dim(second_all, start_feature, sub_block.shape[0])
        coeffs = contract_last(numer_grad, sub_block) * multiplicity(first_index, second_index)
        return summed + spread_back(coeffs, stacked_query, first_index, second_index)

    remote_grad = over_blocks(
        zero_rows, lax.all_gather(prefix, "head", axis=0, tiled=True), feat_here, add_query_grad
    )
    query_grad = (
        (query_local + remote_grad)
        .astype(jnp.bfloat16)
        .reshape(heads_here, row_count, head_width)
        .transpose(1, 0, 2)
        .reshape(row_count, group_rows // row_count * head_width)
    )
    all_grad = lax.all_gather(numer_grad, "head", axis=0, tiled=True)

    def add_dual(position, summed):
        picked_query = lax.dynamic_slice_in_dim(all_query, position * row_count, row_count)
        picked_grad = lax.dynamic_slice_in_dim(all_grad, position * row_count, row_count)
        features = query_features(picked_query, first_mine, second_mine)
        return summed + contract_rows(features, picked_grad)

    dual_local = lax.fori_loop(
        0, all_query.shape[0] // row_count, add_dual, jnp.zeros_like(local_state)
    )
    suffix = prefix_3(dual_local, "seq", jnp.add, jnp.zeros_like(dual_local)).astype(jnp.bfloat16)
    key_coeffs = contract_last(value_rows, suffix)
    key_part = key_local + spread_back(key_coeffs, key_rows, first_mine, second_mine)
    value_part = value_local + jnp.dot(key_features, suffix, preferred_element_type=jnp.float32)
    key_sum, value_sum = (
        lax.psum(key_part.astype(jnp.bfloat16), "head").astype(jnp.float32),
        lax.psum(value_part.astype(jnp.bfloat16), "head").astype(jnp.float32),
    )
    return (attended, query_grad, key_sum.astype(jnp.bfloat16), value_sum.astype(jnp.bfloat16))


def solution(mesh):
    placed = (P("seq", "head"), P("seq", None), P("seq", None), P("seq", "head"))
    return jax.shard_map(
        local,
        mesh=mesh,
        in_specs=placed,
        out_specs=(P("seq", "head"), P("seq", "head"), P("seq", None), P("seq", None)),
        check_vma=False,
    )
```

profile of v0, /device:TPU:0, one launch (start us, length us, event | category | flops | bytes accessed | tf_op | source)
XLA Modules:
  0.0 308.9 jit_solution(13314639366563086069)
XLA Ops:
  14.9 17.3 %all_gather.21 = bf16[2048,128]{1,0:T(8,128)(2,1)S(1)} all-gather(bf16[512,128]{1,0:T(8,128)(2,1)S(1)} %bitcast.124), channel_id=1, replica_groups=mesh['seq'=8,'head'=4] {'head'}, dimensions={0}, use_global_device_ids=true | all-gather | bytes 655360 | tf_op jit(solution)/shard_map/all_gather | solution.py:133
  32.2 39.1 %all-gather.8.cloned.1.call-done = f32[16512,128]{1,0:T(8,128)} async-done(((f32[2064,128]{1,0:T(8,128)}), f32[16512,128]{1,0:T(8,128)}) %all-gather.8.cloned.1.call-update) | async-done | bytes 8454160 | tf_op jit(solution)/shard_map/all_gather | solution.py:12
  71.3 12.1 %while.72 = (s32[]{:T(128)}, f32[2064,128]{1,0:T(8,128)S(1)}, s32[]{:T(128)}, f32[8,2064,128]{2,1,0:T(8,128)}, s32[]{:T(128)}, /*index=5*/s32[]{:T(128)}) while((s32[]{:T(128)}, f32[2064,128]{1,0:T(8,128)S(1)}, s32[]{:T(128)}, f32[8,2064,128]{2,1,0:T(8,128)}, s32[]{:T(128)}, /*index=5*/s32[]{:T(128)}) %tuple.182), condition=%wide.region_1.2_spmd.clone, body=%wide.region_0.1_spmd.clone.sunk | while | flops 792580 | bytes 3170397 | solution.py:20
  83.5 31.0 %while.71 = (s32[]{:T(128)}, bf16[4,512,128]{2,1,0:T(8,128)(2,1)S(1)}, s32[4]{0:T(128)S(1)}, bf16[2048,128]{1,0:T(8,128)(2,1)S(1)}, s32[2064]{0:T(1024)S(1)}, /*...) while((s32[]{:T(128)}, ...), condition=%wide.region_3.4_spmd, body=%wide.region_2.3_spmd.sunk | while | flops 815298560 | bytes 9554187 | solution.py:140
  84.8 2.8 fusion.123
  87.6 3.7 %fusion.124 = bf16[4,512,128]{2,1,0:T(8,128)(2,1)S(1)} fusion(bf16[4,512,128]{2,1,0:T(8,128)(2,1)S(1)} %get-tuple-element.892, s32[]{:T(128)} %get-tuple-element.891, bf16[2064,128]{1,0:T(8,128)(2,1)S(1)} %get-tuple-element.910, f32[512,2064]{1,0:T(8,128)} %fusion.123, f32[2064]{0:T(1024)S(1)} %select_reduce_fusion.4, ...), kind=kOutput, calls=%fused_computation.29.clone.1 | convolution fusion | flops 544499712 | bytes 5173256 | tf_op jit(solution)/shard_map/while/body/eval_jaxpr/dot_general | solution.py:138
  92.5 2.8 fusion.123
  95.4 3.7 %fusion.124 = bf16[4,512,128]{2,1,0:T(8,128)(2,1)S(1)} fusion(bf16[4,512,128]{2,1,0:T(8,128)(2,1)S(1)} %get-tuple-element.892, s32[]{:T(128)} %get-tuple-element.891, bf16[2064,128]{1,0:T(8,128)(2,1)S(1)} %get-tuple-element.910, f32[512,2064]{1,0:T(8,128)} %fusion.123, f32[2064]{0:T(1024)S(1)} %select_reduce_fusion.4, ...), kind=kOutput, calls=%fused_computation.29.clone.1 | convolution fusion | flops 544499712 | bytes 5173256 | tf_op jit(solution)/shard_map/while/body/eval_jaxpr/dot_general | solution.py:138
  100.3 2.8 fusion.123
  103.1 3.7 %fusion.124 = bf16[4,512,128]{2,1,0:T(8,128)(2,1)S(1)} fusion(bf16[4,512,128]{2,1,0:T(8,128)(2,1)S(1)} %get-tuple-element.892, s32[]{:T(128)} %get-tuple-element.891, bf16[2064,128]{1,0:T(8,128)(2,1)S(1)} %get-tuple-element.910, f32[512,2064]{1,0:T(8,128)} %fusion.123, f32[2064]{0:T(1024)S(1)} %select_reduce_fusion.4, ...), kind=kOutput, calls=%fused_computation.29.clone.1 | convolution fusion | flops 544499712 | bytes 5173256 | tf_op jit(solution)/shard_map/while/body/eval_jaxpr/dot_general | solution.py:138
  108.0 2.8 fusion.123
  110.9 3.7 %fusion.124 = bf16[4,512,128]{2,1,0:T(8,128)(2,1)S(1)} fusion(bf16[4,512,128]{2,1,0:T(8,128)(2,1)S(1)} %get-tuple-element.892, s32[]{:T(128)} %get-tuple-element.891, bf16[2064,128]{1,0:T(8,128)(2,1)S(1)} %get-tuple-element.910, f32[512,2064]{1,0:T(8,128)} %fusion.123, f32[2064]{0:T(1024)S(1)} %select_reduce_fusion.4, ...), kind=kOutput, calls=%fused_computation.29.clone.1 | convolution fusion | flops 544499712 | bytes 5173256 | tf_op jit(solution)/shard_map/while/body/eval_jaxpr/dot_general | solution.py:138
  116.2 21.2 %reduce-scatter.2.cloned.1.call-done = bf16[512,128]{1,0:T(8,128)(2,1)} async-done(((bf16[2048,128]{1,0:T(8,128)(2,1)}), bf16[512,128]{1,0:T(8,128)(2,1)}) %reduce-scatter.2.cloned.1.call-update) | async-done | bytes 131088 | tf_op jit(solution)/shard_map/reduce_scatter | solution.py:143
  140.5 19.8 %all_gather.25 = bf16[2048,128]{1,0:T(8,128)(2,1)} all-gather(bf16[512,128]{1,0:T(8,128)(2,1)S(1)} %get-tuple-element.918), channel_id=1, replica_groups=mesh['seq'=8,'head'=4] {'head'}, dimensions={0}, use_global_device_ids=true | all-gather | bytes 655360 | tf_op jit(solution)/shard_map/all_gather | solution.py:191
  160.4 34.0 %while.73 = (s32[]{:T(128)}, f32[2064,128]{1,0:T(8,128)S(1)}, bf16[2048,128]{1,0:T(8,128)(2,1)S(1)}, s32[2064]{0:T(1024)S(1)}, s32[2064]{0:T(1024)S(1)}, /*index...) while((s32[]{:T(128)}, f32[2064,128]{1,0:T(8,128)S(1)}, ...), condition=%wide.region_10.11_spmd.clone, body=%wide.region_9.10_spmd.clone.sunk | while | flops 204750880 | bytes 4431608 | solution.py:199
  160.7 1.7 convolution_add_fusion.4
  162.9 1.7 convolution_add_fusion.4
  165.0 1.7 convolution_add_fusion.4
  167.1 1.7 convolution_add_fusion.4
  169.3 1.7 convolution_add_fusion.4
  171.4 1.7 convolution_add_fusion.4
  173.5 1.7 convolution_add_fusion.4
  175.7 1.7 convolution_add_fusion.4
  177.8 1.7 convolution_add_fusion.4
  179.9 1.7 convolution_add_fusion.4
  182.0 1.7 convolution_add_fusion.4
  184.2 1.7 convolution_add_fusion.4
  186.3 1.7 convolution_add_fusion.4
  188.4 1.7 convolution_add_fusion.4
  190.5 1.7 convolution_add_fusion.4
  192.7 1.7 convolution_add_fusion.4
  196.6 50.5 %while.75 = (s32[]{:T(128)}, f32[512,128]{1,0:T(8,128)S(1)}, bf16[8256,128]{1,0:T(8,128)(2,1)}, bf16[512,128]{1,0:T(8,128)(2,1)S(1)}, bf16[512,128]{1,0:T(8,128)...) while((s32[]{:T(128)}, f32[512,128]{1,0:T(8,128)S(1)}, ...), condition=%wide.region_8.9_spmd.clone.clone, body=%wide.region_7.8_spmd.sunk.clone.clone.sunk | while | flops 1359732736 | bytes 14750645 | solution.py:97
  196.7 3.8 %convolution_multiply_fusion.7 = f32[2064,512]{1,0:T(8,128)} fusion(bf16[512,128]{1,0:T(8,128)(2,1)S(1)} %get-tuple-element.940, f32[2064]{0:T(1024)S(1)} %compare_select_fusion.2, bf16[8256,128]{1,0:T(8,128)(2,1)} %get-tuple-element.939, s32[]{:T(128)S(6)} %select_n.169), kind=kOutput, calls=%fused_computation.4.clone.1 | convolution fusion | flops 271589376 | bytes 4894788 | tf_op jit(solution)/shard_map/while/body/eval_jaxpr/dot_general | solution.py:86
  200.7 4.5 %fusion.135 = f32[512,128]{1,0:T(8,128)S(1)} fusion(f32[2064,512]{1,0:T(8,128)} %convolution_multiply_fusion.7, bf16[512,128]{1,0:T(8,128)(2,1)S(1)} %get-tuple-element.941, s32[2064]{0:T(1024)S(1)} %dynamic_slice.128, s32[2064]{0:T(1024)S(1)} %dynamic_slice.129), kind=kOutput, calls=%fused_computation.7.clone.1 | convolution fusion | flops 543971328 | bytes 4636800 | tf_op jit(solution)/shard_map/while/body/eval_jaxpr/dot_general | solution.py:74
  205.2 4.3 %fusion.136 = f32[512,128]{1,0:T(8,128)S(1)} fusion(f32[512,128]{1,0:T(8,128)S(1)} %fusion.135, f32[2064,512]{1,0:T(8,128)} %convolution_multiply_fusion.7, bf16[512,128]{1,0:T(8,128)(2,1)S(1)} %get-tuple-element.941, s32[2064]{0:T(1024)S(1)} %dynamic_slice.129, s32[2064]{0:T(1024)S(1)} %dynamic_slice.128, f32[512,128]{1,0:T(8,128)S(1)} %get-tuple-element.927, ...), kind=kOutput, calls=%fused_computation.10.clone.1 | convolution fusion | flops 544167936 | bytes 5161089 | tf_op jit(solution)/shard_map/while/body/eval_jaxpr/dot_general | solution.py:71
  209.5 3.8 %convolution_multiply_fusion.7 = f32[2064,512]{1,0:T(8,128)} fusion(bf16[512,128]{1,0:T(8,128)(2,1)S(1)} %get-tuple-element.940, f32[2064]{0:T(1024)S(1)} %compare_select_fusion.2, bf16[8256,128]{1,0:T(8,128)(2,1)} %get-tuple-element.939, s32[]{:T(128)S(6)} %select_n.169), kind=kOutput, calls=%fused_computation.4.clone.1 | convolution fusion | flops 271589376 | bytes 4894788 | tf_op jit(solution)/shard_map/while/body/eval_jaxpr/dot_general | solution.py:86
  213.5 4.2 %fusion.135 = f32[512,128]{1,0:T(8,128)S(1)} fusion(f32[2064,512]{1,0:T(8,128)} %convolution_multiply_fusion.7, bf16[512,128]{1,0:T(8,128)(2,1)S(1)} %get-tuple-element.941, s32[2064]{0:T(1024)S(1)} %dynamic_slice.128, s32[2064]{0:T(1024)S(1)} %dynamic_slice.129), kind=kOutput, calls=%fused_computation.7.clone.1 | convolution fusion | flops 543971328 | bytes 4636800 | tf_op jit(solution)/shard_map/while/body/eval_jaxpr/dot_general | solution.py:74
  217.7 4.3 %fusion.136 = f32[512,128]{1,0:T(8,128)S(1)} fusion(f32[512,128]{1,0:T(8,128)S(1)} %fusion.135, f32[2064,512]{1,0:T(8,128)} %convolution_multiply_fusion.7, bf16[512,128]{1,0:T(8,128)(2,1)S(1)} %get-tuple-element.941, s32[2064]{0:T(1024)S(1)} %dynamic_slice.129, s32[2064]{0:T(1024)S(1)} %dynamic_slice.128, f32[512,128]{1,0:T(8,128)S(1)} %get-tuple-element.927, ...), kind=kOutput, calls=%fused_computation.10.clone.1 | convolution fusion | flops 544167936 | bytes 5161089 | tf_op jit(solution)/shard_map/while/body/eval_jaxpr/dot_general | solution.py:71
  222.1 3.8 %convolution_multiply_fusion.7 = f32[2064,512]{1,0:T(8,128)} fusion(bf16[512,128]{1,0:T(8,128)(2,1)S(1)} %get-tuple-element.940, f32[2064]{0:T(1024)S(1)} %compare_select_fusion.2, bf16[8256,128]{1,0:T(8,128)(2,1)} %get-tuple-element.939, s32[]{:T(128)S(6)} %select_n.169), kind=kOutput, calls=%fused_computation.4.clone.1 | convolution fusion | flops 271589376 | bytes 4894788 | tf_op jit(solution)/shard_map/while/body/eval_jaxpr/dot_general | solution.py:86
  226.0 4.2 %fusion.135 = f32[512,128]{1,0:T(8,128)S(1)} fusion(f32[2064,512]{1,0:T(8,128)} %convolution_multiply_fusion.7, bf16[512,128]{1,0:T(8,128)(2,1)S(1)} %get-tuple-element.941, s32[2064]{0:T(1024)S(1)} %dynamic_slice.128, s32[2064]{0:T(1024)S(1)} %dynamic_slice.129), kind=kOutput, calls=%fused_computation.7.clone.1 | convolution fusion | flops 543971328 | bytes 4636800 | tf_op jit(solution)/shard_map/while/body/eval_jaxpr/dot_general | solution.py:74
  230.3 4.3 %fusion.136 = f32[512,128]{1,0:T(8,128)S(1)} fusion(f32[512,128]{1,0:T(8,128)S(1)} %fusion.135, f32[2064,512]{1,0:T(8,128)} %convolution_multiply_fusion.7, bf16[512,128]{1,0:T(8,128)(2,1)S(1)} %get-tuple-element.941, s32[2064]{0:T(1024)S(1)} %dynamic_slice.129, s32[2064]{0:T(1024)S(1)} %dynamic_slice.128, f32[512,128]{1,0:T(8,128)S(1)} %get-tuple-element.927, ...), kind=kOutput, calls=%fused_computation.10.clone.1 | convolution fusion | flops 544167936 | bytes 5161089 | tf_op jit(solution)/shard_map/while/body/eval_jaxpr/dot_general | solution.py:71
  234.7 3.8 %convolution_multiply_fusion.7 = f32[2064,512]{1,0:T(8,128)} fusion(bf16[512,128]{1,0:T(8,128)(2,1)S(1)} %get-tuple-element.940, f32[2064]{0:T(1024)S(1)} %compare_select_fusion.2, bf16[8256,128]{1,0:T(8,128)(2,1)} %get-tuple-element.939, s32[]{:T(128)S(6)} %select_n.169), kind=kOutput, calls=%fused_computation.4.clone.1 | convolution fusion | flops 271589376 | bytes 4894788 | tf_op jit(solution)/shard_map/while/body/eval_jaxpr/dot_general | solution.py:86
  238.6 4.2 %fusion.135 = f32[512,128]{1,0:T(8,128)S(1)} fusion(f32[2064,512]{1,0:T(8,128)} %convolution_multiply_fusion.7, bf16[512,128]{1,0:T(8,128)(2,1)S(1)} %get-tuple-element.941, s32[2064]{0:T(1024)S(1)} %dynamic_slice.128, s32[2064]{0:T(1024)S(1)} %dynamic_slice.129), kind=kOutput, calls=%fused_computation.7.clone.1 | convolution fusion | flops 543971328 | bytes 4636800 | tf_op jit(solution)/shard_map/while/body/eval_jaxpr/dot_general | solution.py:74
  242.8 4.3 %fusion.136 = f32[512,128]{1,0:T(8,128)S(1)} fusion(f32[512,128]{1,0:T(8,128)S(1)} %fusion.135, f32[2064,512]{1,0:T(8,128)} %convolution_multiply_fusion.7, bf16[512,128]{1,0:T(8,128)(2,1)S(1)} %get-tuple-element.941, s32[2064]{0:T(1024)S(1)} %dynamic_slice.129, s32[2064]{0:T(1024)S(1)} %dynamic_slice.128, f32[512,128]{1,0:T(8,128)S(1)} %get-tuple-element.927, ...), kind=kOutput, calls=%fused_computation.10.clone.1 | convolution fusion | flops 544167936 | bytes 5161089 | tf_op jit(solution)/shard_map/while/body/eval_jaxpr/dot_general | solution.py:71
  247.3 13.2 %while.74 = (s32[]{:T(128)}, f32[2064,128]{1,0:T(8,128)S(1)}, s32[]{:T(128)}, bf16[8,2064,128]{2,1,0:T(8,128)(2,1)}, s32[]{:T(128)}, /*index=5*/s32[]{:T(128)}, s32[]{:T(128)}, s32[]{:T(128)}) while((s32[]{:T(128)}, f32[2064,128]{1,0:T(8,128)S(1)}, s32[]{:T(128)}, bf16[8,2064,128]{2,1,0:T(8,128)(2,1)}, s32[]{:T(128)}, ...), condition=%wide.region_12.13_spmd.clone, body=%wide.region_11.12_spmd.clone.sunk | while | flops 1056776 | bytes 2642075 | solution.py:34
  247.3 1.6 add_select_fusion.5
  249.0 1.6 add_select_fusion.5
  266.1 33.5 %all-reduce.3.cloned.1.call-done = (bf16[128,128]{1,0:T(8,128)(2,1)}, bf16[128,128]{1,0:T(8,128)(2,1)}) async-done(((bf16[128,128]{1,0:T(8,128)(2,1)}, bf16[128,128]{1,0:T(8,128)(2,1)}), (bf16[128,128]{1,0:T(8,128)(2,1)}, bf16[128,128]{1,0:T(8,128)(2,1)})) %all-reduce.3.cloned.1.call-update) | async-done | bytes 65552 | tf_op jit(solution)/shard_map/psum | solution.py:207
  (157 shorter events, 53.8 us)
Async XLA Ops:
  7.2 7.7 %copy-start = (bf16[128,512]{1,0:T(8,128)(2,1)S(1)}, bf16[128,512]{1,0:T(8,128)(2,1)}, u32[]{:S(2)}) copy-start(bf16[128,512]{1,0:T(8,128)(2,1)} %param.16) | copy-start | bytes 393220
  7.2 2.9 copy-start.13
  7.2 64.1 %all-gather.8.cloned.1.call-start = ((), (), s32[]{:S(2)}) async-start(), calls=%async_computation.3 | async-start | bytes 9510912 | tf_op jit(solution)/shard_map/all_gather | solution.py:12
  10.1 1.5 copy-start.2
  10.1 2.3 copy-start.12
  11.6 0.8 copy-start.4
  13.9 123.5 %reduce-scatter.2.cloned.1.call-start = ((), (), s32[]{:S(2)}) async-start(), calls=%async_computation.1 | async-start | bytes 655360 | tf_op jit(solution)/shard_map/reduce_scatter | solution.py:143
  83.5 32.0 %copy-start.19 = (bf16[128,512]{1,0:T(8,128)(2,1)S(1)}, bf16[128,512]{1,0:T(8,128)(2,1)}, u32[]{:S(2)}) copy-start(bf16[128,512]{1,0:T(8,128)(2,1)} %param.19) | copy-start | bytes 393220
  114.5 0.8 copy-start.16
  114.5 1.3 copy-start.1
  115.4 81.2 %all-gather.6.cloned.1.call-start = ((), (), s32[]{:S(2)}) async-start(), calls=%async_computation.2 | async-start | bytes 2641920 | tf_op jit(solution)/shard_map/all_gather | solution.py:182
  115.5 0.7 copy-start.17
  115.7 24.0 %copy-start.7 = (f32[4,128,128]{2,1,0:T(8,128)}, f32[4,128,128]{2,1,0:T(8,128)S(1)}, u32[]{:S(2)}) copy-start(f32[4,128,128]{2,1,0:T(8,128)S(1)} %fusion.74) | copy-start | bytes 786436
  116.1 131.2 %all-gather.10.cloned.1.call-start = ((), (), s32[]{:S(2)}) async-start(), calls=%async_computation.4 | async-start | bytes 4755456 | tf_op jit(solution)/shard_map/all_gather | solution.py:25
  137.4 2.3 copy-start.9
  194.4 1.2 copy-start.15
  194.4 1.3 copy-start.8
  194.4 1.3 copy-start.18
  195.3 1.1 copy-start.14
  195.3 1.3 copy-start.10
  195.3 1.3 copy-start.11
  195.3 104.2 %all-reduce.3.cloned.1.call-start = ((), (), s32[]{:S(2)}) async-start(), calls=%async_computation.5 | async-start | bytes 131072 | tf_op jit(solution)/shard_map/psum | solution.py:207
  260.5 1.0 copy-start.5
  261.5 1.2 copy-start.3
  262.8 1.2 copy-start.6
Sparse Core Ops, SparseCore 0:
  14.0 57.2 all-gather.7
  115.5 21.8 reduce-scatter.1
  138.9 48.5 all-gather.5
  195.4 35.9 all-gather.9
  265.4 34.0 all-reduce.2
where the time goes:
time: 312 us; the launch traced here: 309 us
  matrix products  117 us (38%)
  waiting for transfers between devices  94.1 us (30%)
  blocking collectives  37.2 us (12%)
  other arithmetic  30.8 us (10%)
  between operations  14.3 us (5%)
  local copies, waits for them, and re-layouts  11.4 us (4%)
  loops' own time  4 us (1%)
    all_gather x1, waiting for transfers between devices, prefix_2(): everything = lax.all_gather(shard, axis)  39.1 us
    psum x1, waiting for transfers between devices, local(): lax.psum(key_part.astype(jnp.bfloat16), 'head').astype(jnp.float32)  33.5 us
    dot_general x17, matrix products, contract_rows(): lax.dot_general(left_side, right_side, (((0,), (0,)), ((), ())), preferre...  28.9 us
    select_n x16, other arithmetic, hop(): return jnp.where(reached, new, before)  24.9 us
    reduce_scatter x1, waiting for transfers between devices, local(): lax.psum_scatter(groups.reshape(group_rows * lax.axis_size('head'), head_...  21.2 us
    all_gather x1, blocking collectives, local(): all_grad = lax.all_gather(numer_grad, 'head', axis=0, tiled=True)  19.8 us
    dot_general x22, matrix products, columns(): jnp.dot(source, picker(picked, source.shape[-1]), preferred_element_type=...  19.3 us
    dot_general x5, matrix products, spread_back(): jnp.dot(right_terms, selector(second_index, head_width), preferred_elemen...  18.5 us
  transfers between devices with their start and end apart: 5, of which 3 were waited for; matrix products, arithmetic and copies ran while one was open for 29% of the time, Pallas kernels for 0%

commit v1 on v0

v1 whole, which is shorter than its diff:
```python
import functools

import jax
import jax.numpy as jnp
from jax import lax
from jax.experimental import pallas as pl
from jax.experimental.pallas import tpu as pltpu
from jax.sharding import PartitionSpec as P

EPSILON = 1e-06


def contract(left, right, left_dim, right_dim):
    return lax.dot_general(
        left, right, (((left_dim,), (right_dim,)), ((), ())), preferred_element_type=jnp.float32
    )


def attention_kernel(
    key_ref, value_ref, query_ref, grad_ref, out_ref, dquery_ref, dkv_ref, score_ref, weight_ref
):
    rows, width = query_ref.shape
    tokens, head_width = key_ref.shape
    heads = width // head_width
    chunk = min(tokens, 2 * rows)
    start = lax.axis_index("seq") * rows

    def stacked(ref):
        return jnp.concatenate(
            [ref[:, h * head_width : (h + 1) * head_width] for h in range(heads)], axis=0
        )

    query = stacked(query_ref)
    key_place = lax.broadcasted_iota(jnp.int32, (chunk, heads * rows), 0)
    query_place = lax.broadcasted_iota(jnp.int32, (chunk, heads * rows), 1) % rows
    ahead = key_place - query_place
    numerator = jnp.zeros((head_width, heads * rows), jnp.float32)
    for at in range(0, tokens, chunk):
        part = slice(at, at + chunk)
        score = contract(key_ref[part, :], query, 1, 1)
        score = jnp.where(ahead <= start - at, score, 0.0)
        weight = (score * score).astype(jnp.bfloat16)
        score_ref[part, :] = score
        weight_ref[part, :] = weight
        numerator = numerator + contract(value_ref[part, :], weight, 0, 0)
    numerator = numerator.T
    root_mean = jnp.sqrt(jnp.mean(numerator * numerator, axis=-1, keepdims=True) + EPSILON)
    normed = numerator / root_mean
    grad = stacked(grad_ref).astype(jnp.float32)
    numer_grad = (
        (grad - normed * jnp.mean(grad * normed, axis=-1, keepdims=True)) / root_mean
    ).astype(jnp.bfloat16)
    attended = normed.astype(jnp.bfloat16)
    dquery = jnp.zeros((head_width, heads * rows), jnp.float32)
    for at in range(0, tokens, chunk):
        part = slice(at, at + chunk)
        value_dots = contract(value_ref[part, :], numer_grad, 1, 1)
        coefficient = (2.0 * score_ref[part, :] * value_dots).astype(jnp.bfloat16)
        dquery = dquery + contract(key_ref[part, :], coefficient, 0, 0)
        dkv_ref[part, :head_width] = contract(coefficient, query, 1, 0).astype(jnp.bfloat16)
        dkv_ref[part, head_width:] = contract(weight_ref[part, :], numer_grad, 1, 0).astype(
            jnp.bfloat16
        )
    dquery = dquery.T.astype(jnp.bfloat16)
    for h in range(heads):
        cols = slice(h * head_width, (h + 1) * head_width)
        out_ref[:, cols] = attended[h * rows : (h + 1) * rows, :]
        dquery_ref[:, cols] = dquery[h * rows : (h + 1) * rows, :]


def local(query_rows, key_rows, value_rows, out_grad):
    rows, head_width = key_rows.shape
    blocks, head_axis = lax.axis_size("seq"), lax.axis_size("head")
    tokens = rows * blocks
    columns = query_rows.shape[1] // head_width * rows
    keys = lax.all_gather(key_rows, "seq", axis=0, tiled=True)
    values = lax.all_gather(value_rows, "seq", axis=0, tiled=True)
    vmem = pl.BlockSpec(memory_space=pltpu.VMEM)
    attended, query_grad, partial = pl.pallas_call(
        attention_kernel,
        out_shape=(
            jax.ShapeDtypeStruct(query_rows.shape, jnp.bfloat16),
            jax.ShapeDtypeStruct(query_rows.shape, jnp.bfloat16),
            jax.ShapeDtypeStruct((tokens, 2 * head_width), jnp.bfloat16),
        ),
        in_specs=[vmem] * 4,
        out_specs=(vmem,) * 3,
        scratch_shapes=[
            pltpu.VMEM((tokens, columns), jnp.float32),
            pltpu.VMEM((tokens, columns), jnp.bfloat16),
        ],
        name="attention",
    )(keys, values, query_rows, out_grad)
    pieces = lax.all_to_all(partial.reshape(blocks, rows, 2 * head_width), "seq", 0, 0)
    summed = jnp.sum(pieces.astype(jnp.float32), axis=0)
    sent = summed.astype(jnp.bfloat16)
    for step in range(1, head_axis):
        ring = [(i, (i + step) % head_axis) for i in range(head_axis)]
        summed = summed + lax.ppermute(sent, "head", ring).astype(jnp.float32)
    summed = summed.astype(jnp.bfloat16)
    return (attended, query_grad, summed[:, :head_width], summed[:, head_width:])


def solution(mesh):
    placed = (P("seq", "head"), P("seq", None), P("seq", None), P("seq", "head"))
    return jax.shard_map(
        local,
        mesh=mesh,
        in_specs=placed,
        out_specs=(P("seq", "head"), P("seq", "head"), P("seq", None), P("seq", None)),
        check_vma=False,
    )
```

time: 312 us -> 51.4 us (0.16)
  matrix products: 117 us -> 0 us
  waiting for transfers between devices: 94.1 us -> 5.05 us
  other arithmetic: 30.8 us -> 0.11 us
  between operations: 14.3 us -> 0.66 us
  local copies, waits for them, and re-layouts: 11.4 us -> 0.64 us
  Pallas kernels: 0 us -> 4.8 us
  starting transfers between devices: 0.39 us -> 4.67 us
  loops' own time: 4 us -> 0 us
    dot_general x65 -> x0, matrix products: 117 us -> none  [the longest x17 28.9 us: contract_rows(): lax.dot_general(left_side, right_side, (((0,), (0,)), ((), ())), preferre...]
    all_gather x3 -> x0, waiting for transfers between devices: 39.1 us -> none  [the longest x1 39.1 us: prefix_2(): everything = lax.all_gather(shard, axis)]
    psum x1 -> x0, waiting for transfers between devices: 33.5 us -> none  [local(): lax.psum(key_part.astype(jnp.bfloat16), 'head').astype(jnp.float32)]
    select_n x40 -> x0, other arithmetic: 25.9 us -> none  [the longest x16 24.9 us: hop(): return jnp.where(reached, new, before)]
    reduce_scatter x1 -> x0, waiting for transfers between devices: 21.2 us -> none  [local(): lax.psum_scatter(groups.reshape(group_rows * lax.axis_size('head'), head_...]
    all_gather x2, blocking collectives: 37.2 us -> 22 us  [the longest x1 12.6 us: local(): keys = lax.all_gather(key_rows, 'seq', axis=0, tiled=True)]
    all_to_all x0 -> x1, blocking collectives: none -> 13.1 us  [local(): lax.all_to_all(partial.reshape(blocks, rows, 2 * head_width), 'seq', 0, 0)]
    unnamed x42 -> x2, local copies, waits for them, and re-layouts: 5.89 us -> 0.01 us
  transfers between devices with their start and end apart: 5 -> 3, of which waited for: 3 -> 3; matrix products, arithmetic and copies ran while one was open for 29% -> 0% of each run, Pallas kernels for 0% -> 0%
where the time goes in v1:
time: 51.4 us; the launch traced here: 51 us
  blocking collectives  35.1 us (68%)
  waiting for transfers between devices  5.05 us (10%)
  Pallas kernels  4.8 us (9%)
  starting transfers between devices  4.67 us (9%)
  between operations  0.66 us (1%)
  local copies, waits for them, and re-layouts  0.64 us (1%)
    all_to_all x1, blocking collectives, local(): lax.all_to_all(partial.reshape(blocks, rows, 2 * head_width), 'seq', 0, 0)  13.1 us
    all_gather x1, blocking collectives, local(): keys = lax.all_gather(key_rows, 'seq', axis=0, tiled=True)  12.6 us
    all_gather x1, blocking collectives, local(): values = lax.all_gather(value_rows, 'seq', axis=0, tiled=True)  9.42 us
    ppermute x3, waiting for transfers between devices, local(): summed = summed + lax.ppermute(sent, 'head', ring).astype(jnp.float32)  5.05 us
    pallas_call x1, Pallas kernels, local(): pl.pallas_call(attention_kernel, out_shape=(jax.ShapeDtypeStruct(query_ro...  4.8 us
    ppermute x3, starting transfers between devices, local(): summed = summed + lax.ppermute(sent, 'head', ring).astype(jnp.float32)  4.67 us
  transfers between devices with their start and end apart: 3, of which 3 were waited for; matrix products, arithmetic and copies ran while one was open for 0% of the time, Pallas kernels for 0%

profile of v1, /device:TPU:0, one launch (start us, length us, event | category | flops | bytes accessed | tf_op | source)
XLA Modules:
  0.0 51.0 jit_solution(7246741753033914969)
XLA Ops:
  0.6 0.0 copy-start
  0.6 12.6 %all_gather.6.key_ref = bf16[1024,128]{1,0:T(8,128)(2,1)} all-gather(bf16[128,128]{1,0:T(8,128)(2,1)} %param.5), channel_id=1, replica_groups=mesh['seq'=8,'head'=4] {'seq'}, dimensions={0}, use_global_device_ids=true | all-gather | bytes 294912 | tf_op jit(solution)/shard_map/all_gather | solution.py:76
  13.2 0.0 copy-done
  13.2 9.4 %all_gather.7.value_ref = bf16[1024,128]{1,0:T(8,128)(2,1)} all-gather(bf16[128,128]{1,0:T(8,128)(2,1)S(1)} %copy-done), channel_id=1, replica_groups=mesh['seq'=8,'head'=4] {'seq'}, dimensions={0}, use_global_device_ids=true | all-gather | bytes 294912 | tf_op jit(solution)/shard_map/all_gather | solution.py:77
  22.6 4.8 %attention.1 = (bf16[128,512]{1,0:T(8,128)(2,1)}, bf16[128,512]{1,0:T(8,128)(2,1)}, bf16[1024,256]{1,0:T(8,128)(2,1)}) custom-call(bf16[1024,128]{1,0:T(8,128)(2,1)} %all_gather.6.key_ref, bf16[1024,128]{1,0:T(8,128)(2,1)} %all_gather.7.value_ref, bf16[128,512]{1,0:T(8,128)(2,1)} %query_ref.1, bf16[128,512]{1,0:T(8,128)(2,1)} %grad_ref.1), custom_call_target="tpu_custom_call" | custom-call | tf_op jit(solution)/shard_map/attention/pallas_call | solution.py:79
  27.4 13.1 %all_to_all.5 = bf16[8,128,256]{2,1,0:T(8,128)(2,1)S(1)} all-to-all(bf16[8,128,256]{2,1,0:T(8,128)(2,1)} %bitcast.1), channel_id=1, replica_groups=mesh['seq'=8,'head'=4] {'seq'}, dimensions={0} | all-to-all | bytes 1048576 | tf_op jit(solution)/shard_map/all_to_all | solution.py:94
  40.6 0.1 convert_reduce_fusion
  40.6 3.7 %collective-permute-start.2 = (bf16[128,256]{1,0:T(8,128)(2,1)S(1)}, bf16[128,256]{1,0:T(8,128)(2,1)S(1)}, u32[]{:S(2)}, u32[]{:S(2)}) collective-permute-start(bf16[128,256]{1,0:T(8,128)(2,1)S(1)} %convert_element_type.19), channel_id=1, source_target_pairs={{0,3},{1,0},{2,1},{3,2},{4,7},{5,4},{6,5},{7,6},{8,11},{9,8},{10,9... | collective-permute-start | bytes 196616 | tf_op jit(solution)/shard_map/ppermute | solution.py:99
  44.3 0.0 collective-permute-start.1
  44.3 1.0 %collective-permute-start = (bf16[128,256]{1,0:T(8,128)(2,1)S(1)}, bf16[128,256]{1,0:T(8,128)(2,1)S(1)}, u32[]{:S(2)}, u32[]{:S(2)}) collective-permute-start(bf16[128,256]{1,0:T(8,128)(2,1)S(1)} %convert_element_type.19), channel_id=1, source_target_pairs={{0,1},{1,2},{2,3},{3,0},{4,5},{5,6},{6,7},{7,4},{8,9},{9,10},{10,1... | collective-permute-start | bytes 196616 | tf_op jit(solution)/shard_map/ppermute | solution.py:99
  45.3 1.2 %collective-permute-done.2 = bf16[128,256]{1,0:T(8,128)(2,1)S(1)} collective-permute-done((bf16[128,256]{1,0:T(8,128)(2,1)S(1)}, bf16[128,256]{1,0:T(8,128)(2,1)S(1)}, u32[]{:S(2)}, u32[]{:S(2)}) %collective-permute-start.2) | collective-permute-done | bytes 65568 | tf_op jit(solution)/shard_map/ppermute | solution.py:99
  46.5 3.1 %collective-permute-done.1 = bf16[128,256]{1,0:T(8,128)(2,1)S(1)} collective-permute-done((bf16[128,256]{1,0:T(8,128)(2,1)S(1)}, bf16[128,256]{1,0:T(8,128)(2,1)S(1)}, u32[]{:S(2)}, u32[]{:S(2)}) %collective-permute-start.1) | collective-permute-done | bytes 65568 | tf_op jit(solution)/shard_map/ppermute | solution.py:99
  49.6 0.8 %collective-permute-done = bf16[128,256]{1,0:T(8,128)(2,1)S(1)} collective-permute-done((bf16[128,256]{1,0:T(8,128)(2,1)S(1)}, bf16[128,256]{1,0:T(8,128)(2,1)S(1)}, u32[]{:S(2)}, u32[]{:S(2)}) %collective-permute-start) | collective-permute-done | bytes 65568 | tf_op jit(solution)/shard_map/ppermute | solution.py:99
  50.4 0.6 %fusion = (bf16[128,128]{1,0:T(8,128)(2,1)}, bf16[128,128]{1,0:T(8,128)(2,1)}) fusion(bf16[128,256]{1,0:T(8,128)(2,1)S(1)} %add_convert_fusion), kind=kLoop, calls=%fused_computation.2 | loop fusion | bytes 131072 | tf_op jit(solution)/shard_map/slice | solution.py:101
  (2 shorter events, 0.0 us)
Async XLA Ops:
  0.6 12.6 %copy-start = (bf16[128,128]{1,0:T(8,128)(2,1)S(1)}, bf16[128,128]{1,0:T(8,128)(2,1)}, u32[]{:S(2)}) copy-start(bf16[128,128]{1,0:T(8,128)(2,1)} %param.6) | copy-start | bytes 98308
  40.6 5.9 %collective-permute-start.2 = (bf16[128,256]{1,0:T(8,128)(2,1)S(1)}, bf16[128,256]{1,0:T(8,128)(2,1)S(1)}, u32[]{:S(2)}, u32[]{:S(2)}) collective-permute-start(bf16[128,256]{1,0:T(8,128)(2,1)S(1)} %convert_element_type.19), channel_id=1, source_target_pairs={{0,3},{1,0},{2,1},{3,2},{4,7},{5,4},{6,5},{7,6},{8,11},{9,8},{10,9... | collective-permute-start | bytes 196616 | tf_op jit(solution)/shard_map/ppermute | solution.py:99
  44.3 5.3 %collective-permute-start.1 = (bf16[128,256]{1,0:T(8,128)(2,1)S(1)}, bf16[128,256]{1,0:T(8,128)(2,1)S(1)}, u32[]{:S(2)}, u32[]{:S(2)}) collective-permute-start(bf16[128,256]{1,0:T(8,128)(2,1)S(1)} %convert_element_type.19), channel_id=1, source_target_pairs={{0,2},{1,3},{2,0},{3,1},{4,6},{5,7},{6,4},{7,5},{8,10},{9,11},{10,... | collective-permute-start | bytes 196616 | tf_op jit(solution)/shard_map/ppermute | solution.py:99
  44.3 6.1 %collective-permute-start = (bf16[128,256]{1,0:T(8,128)(2,1)S(1)}, bf16[128,256]{1,0:T(8,128)(2,1)S(1)}, u32[]{:S(2)}, u32[]{:S(2)}) collective-permute-start(bf16[128,256]{1,0:T(8,128)(2,1)S(1)} %convert_element_type.19), channel_id=1, source_target_pairs={{0,1},{1,2},{2,3},{3,0},{4,5},{5,6},{6,7},{7,4},{8,9},{9,10},{10,1... | collective-permute-start | bytes 196616 | tf_op jit(solution)/shard_map/ppermute | solution.py:99

commit v2 on v1

v2 whole, which is shorter than its diff:
```python
import functools

import jax
import jax.numpy as jnp
from jax import lax
from jax.experimental import pallas as pl
from jax.experimental.pallas import tpu as pltpu
from jax.sharding import PartitionSpec as P

EPSILON = 1e-06
VMEM_LIMIT = 16 * 1024 * 1024


def contract(left, right, left_dim, right_dim):
    return lax.dot_general(
        left, right, (((left_dim,), (right_dim,)), ((), ())), preferred_element_type=jnp.float32
    )


def call(kernel, outs, *operands, name):
    vmem = pl.BlockSpec(memory_space=pltpu.VMEM)
    operands = [pltpu.with_memory_space_constraint(x, pltpu.VMEM) for x in operands]
    return pl.pallas_call(
        kernel,
        out_shape=[pltpu.VMEM(shape, kind) for shape, kind in outs],
        in_specs=[vmem] * len(operands),
        out_specs=[vmem] * len(outs),
        compiler_params=pltpu.CompilerParams(vmem_limit_bytes=VMEM_LIMIT),
        name=name,
    )(*operands)


def load_kernel(query_hbm, key_hbm, value_hbm, grad_hbm, pair_ref, query_ref, grad_ref, sems):
    rows, head_width = key_hbm.shape
    copies = [(key_hbm, pair_ref.at[:, :head_width]), (value_hbm, pair_ref.at[:, head_width:])]
    for h in range(query_hbm.shape[1] // head_width):
        columns, below = pl.ds(h * head_width, head_width), pl.ds(h * rows, rows)
        copies.append((query_hbm.at[:, columns], query_ref.at[below, :]))
        copies.append((grad_hbm.at[:, columns], grad_ref.at[below, :]))
    copies = [
        pltpu.make_async_copy(source, target, sems.at[i])
        for i, (source, target) in enumerate(copies)
    ]
    for copy in copies:
        copy.start()
    for copy in copies:
        copy.wait()


def load(query_rows, key_rows, value_rows, out_grad):
    rows, head_width = key_rows.shape
    heads = query_rows.shape[1] // head_width
    stack = pltpu.VMEM((heads * rows, head_width), query_rows.dtype)
    operands = [
        pltpu.with_memory_space_constraint(x, pltpu.HBM)
        for x in (query_rows, key_rows, value_rows, out_grad)
    ]
    return pl.pallas_call(
        load_kernel,
        out_shape=[pltpu.VMEM((rows, 2 * head_width), key_rows.dtype), stack, stack],
        in_specs=[pl.BlockSpec(memory_space=pltpu.HBM)] * 4,
        out_specs=[pl.BlockSpec(memory_space=pltpu.VMEM)] * 3,
        scratch_shapes=[pltpu.SemaphoreType.DMA((2 + 2 * heads,))],
        compiler_params=pltpu.CompilerParams(vmem_limit_bytes=VMEM_LIMIT),
        name="load",
    )(*operands)


def halves(refs):
    width = refs[0].shape[1] // 2
    return (
        jnp.concatenate([ref[:, :width] for ref in refs], axis=0),
        jnp.concatenate([ref[:, width:] for ref in refs], axis=0),
    )


def forward_kernel(masks, *refs):
    count = len(masks)
    slots, (query_ref, grad_ref) = refs[:count], refs[count : count + 2]
    score_refs, (numer_ref, out_ref) = refs[count + 2 : -2], refs[-2:]
    rows, head_width = slots[0].shape[0], slots[0].shape[1] // 2
    own = lax.axis_index("seq")
    query = query_ref[...]
    columns = query.shape[0]
    numerator = jnp.zeros((head_width, columns), jnp.float32)
    half = count // len(score_refs)
    for i, score_ref in enumerate(score_refs):
        span = slice(i * half, (i + 1) * half)
        keys, values = halves(slots[span])
        score = contract(keys, query, 1, 1)
        pieces = []
        for j, mask in enumerate(masks[span]):
            piece = score[j * rows : (j + 1) * rows, :]
            if mask == 0:
                key_place = lax.broadcasted_iota(jnp.int32, (rows, columns), 0)
                query_place = lax.broadcasted_iota(jnp.int32, (rows, columns), 1) % rows
                piece = jnp.where(key_place <= query_place, piece, 0.0)
            else:
                piece = jnp.where((own ^ mask) < own, piece, 0.0)
            pieces.append(piece)
        score = jnp.concatenate(pieces, axis=0)
        score_ref[...] = score
        numerator = numerator + contract(values, (score * score).astype(jnp.bfloat16), 0, 0)
    numerator = numerator.T
    root_mean = jnp.sqrt(jnp.mean(numerator * numerator, axis=-1, keepdims=True) + EPSILON)
    normed = numerator / root_mean
    grad = grad_ref[...].astype(jnp.float32)
    numer_ref[...] = (
        (grad - normed * jnp.mean(grad * normed, axis=-1, keepdims=True)) / root_mean
    ).astype(jnp.bfloat16)
    attended = normed.astype(jnp.bfloat16)
    for h in range(columns // rows):
        out_ref[:, h * head_width : (h + 1) * head_width] = attended[h * rows : (h + 1) * rows, :]


def backward_kernel(*refs):
    slots, (score_ref, numer_ref, query_ref, coefficient_ref, dkv_ref) = refs[:-5], refs[-5:]
    rows, head_width = slots[0].shape[0], slots[0].shape[1] // 2
    _, values = halves(slots)
    query = query_ref[...]
    numer_grad = numer_ref[...]
    score = score_ref[...]
    coefficient = (2.0 * score * contract(values, numer_grad, 1, 1)).astype(jnp.bfloat16)
    coefficient_ref[...] = coefficient
    dkv_ref[:, :head_width] = contract(coefficient, query, 1, 0).astype(jnp.bfloat16)
    weight = (score * score).astype(jnp.bfloat16)
    dkv_ref[:, head_width:] = contract(weight, numer_grad, 1, 0).astype(jnp.bfloat16)


def query_kernel(*refs):
    slots, coefficient_refs, dquery_ref = refs[:-3], refs[-3:-1], refs[-1]
    rows, head_width = slots[0].shape[0], slots[0].shape[1] // 2
    half = len(slots) // 2
    dquery = 0.0
    for i, coefficient_ref in enumerate(coefficient_refs):
        keys, _ = halves(slots[i * half : (i + 1) * half])
        dquery = dquery + contract(keys, coefficient_ref[...], 0, 0)
    dquery = dquery.T.astype(jnp.bfloat16)
    for h in range(dquery.shape[0] // rows):
        dquery_ref[:, h * head_width : (h + 1) * head_width] = dquery[h * rows : (h + 1) * rows, :]


def partner(array, axis, mask):
    return lax.ppermute(array, axis, [(i, i ^ mask) for i in range(lax.axis_size(axis))])


def local(query_rows, key_rows, value_rows, out_grad):
    rows, head_width = key_rows.shape
    blocks, head_axis = lax.axis_size("seq"), lax.axis_size("head")
    columns = query_rows.shape[1] // head_width * rows
    evens = tuple(range(0, blocks, 2))
    half = rows * len(evens)
    pair, query, grad = load(query_rows, key_rows, value_rows, out_grad)
    even = [pair] + [partner(pair, "seq", m) for m in evens[1:]]
    odd = [partner(block, "seq", 1) for block in even]
    masks = evens + tuple(m ^ 1 for m in evens)
    score_even, score_odd, numer_grad, attended = call(
        functools.partial(forward_kernel, masks),
        [((half, columns), jnp.float32)] * 2
        + [((columns, head_width), jnp.bfloat16), (query_rows.shape, jnp.bfloat16)],
        *even,
        *odd,
        query,
        grad,
        name="forward",
    )
    outs = [((half, columns), jnp.bfloat16), ((half, 2 * head_width), jnp.bfloat16)]
    coefficient_odd, away = call(
        backward_kernel, outs, *odd, score_odd, numer_grad, query, name="backward_odd"
    )
    swapped = partner(away, "seq", 1)
    coefficient_even, kept = call(
        backward_kernel, outs, *even, score_even, numer_grad, query, name="backward_even"
    )
    chip = kept.astype(jnp.float32) + swapped.astype(jnp.float32)
    chip = chip.reshape(len(evens), rows, 2 * head_width)
    summed = chip[0]
    arrived = [
        partner(chip[i].astype(jnp.bfloat16), "seq", evens[i]) for i in range(1, len(evens))
    ]
    for piece in arrived:
        summed = summed + piece.astype(jnp.float32)
    (query_grad,) = call(
        query_kernel,
        [(query_rows.shape, jnp.bfloat16)],
        *even,
        *odd,
        coefficient_even,
        coefficient_odd,
        name="query_grad",
    )
    sent = summed.astype(jnp.bfloat16)
    for mask in range(1, head_axis):
        summed = summed + partner(sent, "head", mask).astype(jnp.float32)
    summed = summed.astype(jnp.bfloat16)
    return (attended, query_grad, summed[:, :head_width], summed[:, head_width:])


def solution(mesh):
    placed = (P("seq", "head"), P("seq", None), P("seq", None), P("seq", "head"))
    return jax.shard_map(
        local,
        mesh=mesh,
        in_specs=placed,
        out_specs=(P("seq", "head"), P("seq", "head"), P("seq", None), P("seq", None)),
        check_vma=False,
    )
```

time: 51.4 us -> 32.7 us (0.64)
  blocking collectives: 35.1 us -> 0 us
  starting transfers between devices: 4.67 us -> 12.9 us
  waiting for transfers between devices: 5.05 us -> 13.2 us
  local copies, waits for them, and re-layouts: 0.64 us -> 1.96 us
  Pallas kernels: 4.8 us -> 3.59 us
    all_gather x2 -> x0, blocking collectives: 22 us -> none  [the longest x1 12.6 us: local(): keys = lax.all_gather(key_rows, 'seq', axis=0, tiled=True)]
    all_to_all x1 -> x0, blocking collectives: 13.1 us -> none  [local(): lax.all_to_all(partial.reshape(blocks, rows, 2 * head_width), 'seq', 0, 0)]
    ppermute x3 -> x14, starting transfers between devices: 4.67 us -> 12.9 us  [partner(): lax.ppermute(array, axis, [(i, i ^ mask) for i in range(lax.axis_size(axi...]
    ppermute x3 -> x14, waiting for transfers between devices: 5.05 us -> 13.2 us  [partner(): lax.ppermute(array, axis, [(i, i ^ mask) for i in range(lax.axis_size(axi...]
    unnamed x2, local copies, waits for them, and re-layouts: 0.01 us -> 1.31 us
    pallas_call x1 -> x5, Pallas kernels: 4.8 us -> 3.59 us  [the longest x4 2.59 us: call(): pl.pallas_call(kernel, out_shape=[pltpu.VMEM(shape, kind) for shape, kind...]
  transfers between devices with their start and end apart: 3 -> 14, of which waited for: 3 -> 11; matrix products, arithmetic and copies ran while one was open for 0% -> 4% of each run, Pallas kernels for 0% -> 3%
where the time goes in v2:
time: 32.7 us; the launch traced here: 32.5 us
  waiting for transfers between devices  13.2 us (40%)
  starting transfers between devices  12.9 us (39%)
  Pallas kernels  3.59 us (11%)
  local copies, waits for them, and re-layouts  1.96 us (6%)
  between operations  0.69 us (2%)
    ppermute x14, waiting for transfers between devices, partner(): lax.ppermute(array, axis, [(i, i ^ mask) for i in range(lax.axis_size(axi...  13.2 us
    ppermute x14, starting transfers between devices, partner(): lax.ppermute(array, axis, [(i, i ^ mask) for i in range(lax.axis_size(axi...  12.9 us
    pallas_call x4, Pallas kernels, call(): pl.pallas_call(kernel, out_shape=[pltpu.VMEM(shape, kind) for shape, kind...  2.59 us
    unnamed x2, local copies, waits for them, and re-layouts  1.31 us
    pallas_call x1, Pallas kernels, load(): pl.pallas_call(load_kernel, out_shape=[pltpu.VMEM((rows, 2 * head_width),...  1 us
  transfers between devices with their start and end apart: 14, of which 11 were waited for; matrix products, arithmetic and copies ran while one was open for 4% of the time, Pallas kernels for 3%

profile of v2, /device:TPU:0, one launch (start us, length us, event | category | flops | bytes accessed | tf_op | source)
XLA Modules:
  0.0 32.5 jit_solution(10060775676640084775)
XLA Ops:
  0.6 1.0 %load.1 = (bf16[128,256]{1,0:T(8,128)(2,1)S(1)}, bf16[512,128]{1,0:T(8,128)(2,1)S(1)}, bf16[512,128]{1,0:T(8,128)(2,1)S(1)}) custom-call(bf16[128,512]{1,0:T(8,128)(2,1)} %query_hbm.1, bf16[128,128]{1,0:T(8,128)(2,1)} %key_hbm.1, bf16[128,128]{1,0:T(8,128)(2,1)} %value_hbm.1, bf16[128,512]{1,0:T(8,128)(2,1)} %grad_hbm.1), custom_call_target="tpu_custom_call" | custom-call | tf_op jit(solution)/shard_map/load/pallas_call | solution.py:58
  1.6 4.0 %collective-permute-start.2 = (bf16[128,256]{1,0:T(8,128)(2,1)S(1)}, bf16[128,256]{1,0:T(8,128)(2,1)S(1)}, u32[]{:S(2)}, u32[]{:S(2)}) collective-permute-start(bf16[128,256]{1,0:T(8,128)(2,1)S(1)} %get-tuple-element.15.refs_0_), channel_id=1, source_target_pairs={{0,24},{4,28},{8,16},{12,20},{16,8},{20,12},{24,0},{28,4},{1,25},{... | collective-permute-start | bytes 196616 | tf_op jit(solution)/shard_map/ppermute | solution.py:144
  5.6 0.5 %collective-permute-start.1 = (bf16[128,256]{1,0:T(8,128)(2,1)S(1)}, bf16[128,256]{1,0:T(8,128)(2,1)S(1)}, u32[]{:S(2)}, u32[]{:S(2)}) collective-permute-start(bf16[128,256]{1,0:T(8,128)(2,1)S(1)} %get-tuple-element.15.refs_0_), channel_id=1, source_target_pairs={{0,16},{4,20},{8,24},{12,28},{16,0},{20,4},{24,8},{28,12},{1,17},{... | collective-permute-start | bytes 196616 | tf_op jit(solution)/shard_map/ppermute | solution.py:144
  6.1 0.1 collective-permute-start
  6.3 0.0 collective-permute-start.3
  6.3 1.6 %collective-permute-done.2.refs_3_ = bf16[128,256]{1,0:T(8,128)(2,1)S(1)} collective-permute-done((bf16[128,256]{1,0:T(8,128)(2,1)S(1)}, bf16[128,256]{1,0:T(8,128)(2,1)S(1)}, u32[]{:S(2)}, u32[]{:S(2)}) %collective-permute-start.2) | collective-permute-done | bytes 65568 | tf_op jit(solution)/shard_map/ppermute | solution.py:144
  7.9 0.0 collective-permute-start.6
  7.9 2.0 %collective-permute-done.1.refs_2_ = bf16[128,256]{1,0:T(8,128)(2,1)S(1)} collective-permute-done((bf16[128,256]{1,0:T(8,128)(2,1)S(1)}, bf16[128,256]{1,0:T(8,128)(2,1)S(1)}, u32[]{:S(2)}, u32[]{:S(2)}) %collective-permute-start.1) | collective-permute-done | bytes 65568 | tf_op jit(solution)/shard_map/ppermute | solution.py:144
  9.9 0.0 collective-permute-start.5
  9.9 0.5 %collective-permute-done.refs_1_ = bf16[128,256]{1,0:T(8,128)(2,1)S(1)} collective-permute-done((bf16[128,256]{1,0:T(8,128)(2,1)S(1)}, bf16[128,256]{1,0:T(8,128)(2,1)S(1)}, u32[]{:S(2)}, u32[]{:S(2)}) %collective-permute-start) | collective-permute-done | bytes 65568 | tf_op jit(solution)/shard_map/ppermute | solution.py:144
  10.4 0.0 collective-permute-start.4
  10.4 0.0 collective-permute-done.3.refs_4_.refs_0_
  10.4 0.0 collective-permute-done.6.refs_7_.refs_3_
  10.4 0.7 %collective-permute-done.5.refs_6_.refs_2_ = bf16[128,256]{1,0:T(8,128)(2,1)S(1)} collective-permute-done((bf16[128,256]{1,0:T(8,128)(2,1)S(1)}, bf16[128,256]{1,0:T(8,128)(2,1)S(1)}, u32[]{:S(2)}, u32[]{:S(2)}) %collective-permute-start.5) | collective-permute-done | bytes 65568 | tf_op jit(solution)/shard_map/ppermute | solution.py:144
  11.1 0.5 %collective-permute-done.4.refs_5_.refs_1_ = bf16[128,256]{1,0:T(8,128)(2,1)S(1)} collective-permute-done((bf16[128,256]{1,0:T(8,128)(2,1)S(1)}, bf16[128,256]{1,0:T(8,128)(2,1)S(1)}, u32[]{:S(2)}, u32[]{:S(2)}) %collective-permute-start.4) | collective-permute-done | bytes 65568 | tf_op jit(solution)/shard_map/ppermute | solution.py:144
  11.7 1.0 %forward.1 = (f32[512,512]{1,0:T(8,128)S(1)}, f32[512,512]{1,0:T(8,128)S(1)}, bf16[512,128]{1,0:T(8,128)(2,1)S(1)}, bf16[128,512]{1,0:T(8,128)(2,1)S(1)}) custom-call(bf16[128,256]{1,0:T(8,128)(2,1)S(1)} %get-tuple-element.15.refs_0_, bf16[128,256]{1,0:T(8,128)(2,1)S(1)} %collective-permute-done.refs_1_, ...), custom_call_target="tpu_custom_call" | custom-call | tf_op jit(solution)/shard_map/forward/pallas_call | solution.py:23
  12.7 0.6 %backward_odd.1 = (bf16[512,512]{1,0:T(8,128)(2,1)S(1)}, bf16[512,256]{1,0:T(8,128)(2,1)S(1)}) custom-call(bf16[128,256]{1,0:T(8,128)(2,1)S(1)} %collective-permute-done.3.refs_4_.refs_0_, bf16[128,256]{1,0:T(8,128)(2,1)S(1)} %collective-permute-done.4.refs_5_.refs_1_, bf16[128,256]{1,0:T(8,128)(2,1)S(1)} %collective-permute-done.5.refs_6_.refs_2_, ...), custom_call_target="tpu_custom_call" | custom-call | tf_op jit(solution)/shard_map/backward_odd/pallas_call | solution.py:23
  13.3 0.2 collective-permute-start.7
  13.5 0.6 %backward_even.1 = (bf16[512,512]{1,0:T(8,128)(2,1)S(1)}, bf16[512,256]{1,0:T(8,128)(2,1)S(1)}) custom-call(bf16[128,256]{1,0:T(8,128)(2,1)S(1)} %get-tuple-element.15.refs_0_, bf16[128,256]{1,0:T(8,128)(2,1)S(1)} %collective-permute-done.refs_1_, bf16[128,256]{1,0:T(8,128)(2,1)S(1)} %collective-permute-done.1.refs_2_, ...), custom_call_target="tpu_custom_call" | custom-call | tf_op jit(solution)/shard_map/backward_even/pallas_call | solution.py:23
  14.1 0.8 %collective-permute-done.7 = bf16[512,256]{1,0:T(8,128)(2,1)S(1)} collective-permute-done((bf16[512,256]{1,0:T(8,128)(2,1)S(1)}, bf16[512,256]{1,0:T(8,128)(2,1)S(1)}, u32[]{:S(2)}, u32[]{:S(2)}) %collective-permute-start.7) | collective-permute-done | bytes 262176 | tf_op jit(solution)/shard_map/ppermute | solution.py:144
  14.9 0.1 convert_add_fusion
  15.0 0.6 %collective-permute-start.8 = (bf16[128,256]{1,0:T(8,128)(2,1)S(1)}, bf16[128,256]{1,0:T(8,128)(2,1)S(1)}, u32[]{:S(2)}, u32[]{:S(2)}) collective-permute-start(bf16[128,256]{1,0:T(8,128)(2,1)S(1)} %get-tuple-element.28), channel_id=1, source_target_pairs={{0,8},{4,12},{8,0},{12,4},{16,24},{20,28},{24,16},{28,20},{1,9},{5... | collective-permute-start | bytes 196616 | tf_op jit(solution)/shard_map/ppermute | solution.py:144
  15.6 2.4 %collective-permute-start.10 = (bf16[128,256]{1,0:T(8,128)(2,1)S(1)}, bf16[128,256]{1,0:T(8,128)(2,1)S(1)}, u32[]{:S(2)}, u32[]{:S(2)}) collective-permute-start(bf16[128,256]{1,0:T(8,128)(2,1)S(1)} %get-tuple-element.29), channel_id=1, source_target_pairs={{0,24},{4,28},{8,16},{12,20},{16,8},{20,12},{24,0},{28,4},{1,25},{... | collective-permute-start | bytes 196616 | tf_op jit(solution)/shard_map/ppermute | solution.py:144
  18.0 0.5 %collective-permute-start.9 = (bf16[128,256]{1,0:T(8,128)(2,1)S(1)}, bf16[128,256]{1,0:T(8,128)(2,1)S(1)}, u32[]{:S(2)}, u32[]{:S(2)}) collective-permute-start(bf16[128,256]{1,0:T(8,128)(2,1)S(1)} %get-tuple-element.30), channel_id=1, source_target_pairs={{0,16},{4,20},{8,24},{12,28},{16,0},{20,4},{24,8},{28,12},{1,17},{... | collective-permute-start | bytes 196616 | tf_op jit(solution)/shard_map/ppermute | solution.py:144
  18.5 1.1 %collective-permute-done.8 = bf16[128,256]{1,0:T(8,128)(2,1)S(1)} collective-permute-done((bf16[128,256]{1,0:T(8,128)(2,1)S(1)}, bf16[128,256]{1,0:T(8,128)(2,1)S(1)}, u32[]{:S(2)}, u32[]{:S(2)}) %collective-permute-start.8) | collective-permute-done | bytes 65568 | tf_op jit(solution)/shard_map/ppermute | solution.py:144
  19.6 2.0 %collective-permute-done.10 = bf16[128,256]{1,0:T(8,128)(2,1)S(1)} collective-permute-done((bf16[128,256]{1,0:T(8,128)(2,1)S(1)}, bf16[128,256]{1,0:T(8,128)(2,1)S(1)}, u32[]{:S(2)}, u32[]{:S(2)}) %collective-permute-start.10) | collective-permute-done | bytes 65568 | tf_op jit(solution)/shard_map/ppermute | solution.py:144
  21.7 0.9 %collective-permute-done.9 = bf16[128,256]{1,0:T(8,128)(2,1)S(1)} collective-permute-done((bf16[128,256]{1,0:T(8,128)(2,1)S(1)}, bf16[128,256]{1,0:T(8,128)(2,1)S(1)}, u32[]{:S(2)}, u32[]{:S(2)}) %collective-permute-start.9) | collective-permute-done | bytes 65568 | tf_op jit(solution)/shard_map/ppermute | solution.py:144
  22.6 3.7 %collective-permute-start.13 = (bf16[128,256]{1,0:T(8,128)(2,1)S(1)}, bf16[128,256]{1,0:T(8,128)(2,1)S(1)}, u32[]{:S(2)}, u32[]{:S(2)}) collective-permute-start(bf16[128,256]{1,0:T(8,128)(2,1)S(1)} %fusion.2), channel_id=1, source_target_pairs={{0,3},{1,2},{2,1},{3,0},{4,7},{5,6},{6,5},{7,4},{8,11},{9,10},{10,... | collective-permute-start | bytes 196616 | tf_op jit(solution)/shard_map/ppermute | solution.py:144
  26.3 0.0 collective-permute-start.12
  26.3 0.8 %collective-permute-start.11 = (bf16[128,256]{1,0:T(8,128)(2,1)S(1)}, bf16[128,256]{1,0:T(8,128)(2,1)S(1)}, u32[]{:S(2)}, u32[]{:S(2)}) collective-permute-start(bf16[128,256]{1,0:T(8,128)(2,1)S(1)} %fusion.2), channel_id=1, source_target_pairs={{0,1},{1,0},{2,3},{3,2},{4,5},{5,4},{6,7},{7,6},{8,9},{9,8},{10,11... | collective-permute-start | bytes 196616 | tf_op jit(solution)/shard_map/ppermute | solution.py:144
  27.1 0.7 %copy.8 = bf16[128,512]{1,0:T(8,128)(2,1)} copy(bf16[128,512]{1,0:T(8,128)(2,1)S(1)} %get-tuple-element.33) | data formatting | bytes 262144
  27.7 0.4 %query_grad.1 = bf16[128,512]{1,0:T(8,128)(2,1)S(1)} custom-call(bf16[128,256]{1,0:T(8,128)(2,1)S(1)} %get-tuple-element.15.refs_0_, bf16[128,256]{1,0:T(8,128)(2,1)S(1)} %collective-permute-done.refs_1_, bf16[128,256]{1,0:T(8,128)(2,1)S(1)} %collective-permute-done.1.refs_2_, bf16[128,256]{1,0:T(8,128)(2,1)S(1)} %collective-permute-done.2.refs_3_, ...), custom_call_target="tpu_custom_call" | custom-call | tf_op jit(solution)/shard_map/query_grad/pallas_call | solution.py:23
  28.1 0.7 %copy.9 = bf16[128,512]{1,0:T(8,128)(2,1)} copy(bf16[128,512]{1,0:T(8,128)(2,1)S(1)} %query_grad.1) | data formatting | bytes 262144
  28.8 0.7 %collective-permute-done.13 = bf16[128,256]{1,0:T(8,128)(2,1)S(1)} collective-permute-done((bf16[128,256]{1,0:T(8,128)(2,1)S(1)}, bf16[128,256]{1,0:T(8,128)(2,1)S(1)}, u32[]{:S(2)}, u32[]{:S(2)}) %collective-permute-start.13) | collective-permute-done | bytes 65568 | tf_op jit(solution)/shard_map/ppermute | solution.py:144
  29.5 2.3 %collective-permute-done.12 = bf16[128,256]{1,0:T(8,128)(2,1)S(1)} collective-permute-done((bf16[128,256]{1,0:T(8,128)(2,1)S(1)}, bf16[128,256]{1,0:T(8,128)(2,1)S(1)}, u32[]{:S(2)}, u32[]{:S(2)}) %collective-permute-start.12) | collective-permute-done | bytes 65568 | tf_op jit(solution)/shard_map/ppermute | solution.py:144
  31.8 0.0 collective-permute-done.11
  31.8 0.1 add_convert_fusion
  31.9 0.6 %fusion.5 = (bf16[128,128]{1,0:T(8,128)(2,1)}, bf16[128,128]{1,0:T(8,128)(2,1)}) fusion(bf16[128,256]{1,0:T(8,128)(2,1)S(1)} %add_convert_fusion), kind=kLoop, calls=%fused_computation.8 | loop fusion | bytes 131072 | tf_op jit(solution)/shard_map/slice | solution.py:196
  (2 shorter events, 0.0 us)
Async XLA Ops:
  1.6 6.2 %collective-permute-start.2 = (bf16[128,256]{1,0:T(8,128)(2,1)S(1)}, bf16[128,256]{1,0:T(8,128)(2,1)S(1)}, u32[]{:S(2)}, u32[]{:S(2)}) collective-permute-start(bf16[128,256]{1,0:T(8,128)(2,1)S(1)} %get-tuple-element.15.refs_0_), channel_id=1, source_target_pairs={{0,24},{4,28},{8,16},{12,20},{16,8},{20,12},{24,0},{28,4},{1,25},{... | collective-permute-start | bytes 196616 | tf_op jit(solution)/shard_map/ppermute | solution.py:144
  5.6 4.3 %collective-permute-start.1 = (bf16[128,256]{1,0:T(8,128)(2,1)S(1)}, bf16[128,256]{1,0:T(8,128)(2,1)S(1)}, u32[]{:S(2)}, u32[]{:S(2)}) collective-permute-start(bf16[128,256]{1,0:T(8,128)(2,1)S(1)} %get-tuple-element.15.refs_0_), channel_id=1, source_target_pairs={{0,16},{4,20},{8,24},{12,28},{16,0},{20,4},{24,8},{28,12},{1,17},{... | collective-permute-start | bytes 196616 | tf_op jit(solution)/shard_map/ppermute | solution.py:144
  6.1 4.3 %collective-permute-start = (bf16[128,256]{1,0:T(8,128)(2,1)S(1)}, bf16[128,256]{1,0:T(8,128)(2,1)S(1)}, u32[]{:S(2)}, u32[]{:S(2)}) collective-permute-start(bf16[128,256]{1,0:T(8,128)(2,1)S(1)} %get-tuple-element.15.refs_0_), channel_id=1, source_target_pairs={{0,8},{4,12},{8,0},{12,4},{16,24},{20,28},{24,16},{28,20},{1,9},{5... | collective-permute-start | bytes 196616 | tf_op jit(solution)/shard_map/ppermute | solution.py:144
  6.3 4.1 %collective-permute-start.3 = (bf16[128,256]{1,0:T(8,128)(2,1)S(1)}, bf16[128,256]{1,0:T(8,128)(2,1)S(1)}, u32[]{:S(2)}, u32[]{:S(2)}) collective-permute-start(bf16[128,256]{1,0:T(8,128)(2,1)S(1)} %get-tuple-element.15.refs_0_), channel_id=1, source_target_pairs={{0,4},{4,0},{8,12},{12,8},{16,20},{20,16},{24,28},{28,24},{1,5},{5... | collective-permute-start | bytes 196616 | tf_op jit(solution)/shard_map/ppermute | solution.py:144
  7.9 2.5 %collective-permute-start.6 = (bf16[128,256]{1,0:T(8,128)(2,1)S(1)}, bf16[128,256]{1,0:T(8,128)(2,1)S(1)}, u32[]{:S(2)}, u32[]{:S(2)}) collective-permute-start(bf16[128,256]{1,0:T(8,128)(2,1)S(1)} %collective-permute-done.2.refs_3_), channel_id=1, source_target_pairs={{0,4},{4,0},{8,12},{12,8},{16,20},{20,16},{24,28},{28,24},{1,5},{5... | collective-permute-start | bytes 196616 | tf_op jit(solution)/shard_map/ppermute | solution.py:144
  9.9 1.3 %collective-permute-start.5 = (bf16[128,256]{1,0:T(8,128)(2,1)S(1)}, bf16[128,256]{1,0:T(8,128)(2,1)S(1)}, u32[]{:S(2)}, u32[]{:S(2)}) collective-permute-start(bf16[128,256]{1,0:T(8,128)(2,1)S(1)} %collective-permute-done.1.refs_2_), channel_id=1, source_target_pairs={{0,4},{4,0},{8,12},{12,8},{16,20},{20,16},{24,28},{28,24},{1,5},{5... | collective-permute-start | bytes 196616 | tf_op jit(solution)/shard_map/ppermute | solution.py:144
  10.4 1.3 %collective-permute-start.4 = (bf16[128,256]{1,0:T(8,128)(2,1)S(1)}, bf16[128,256]{1,0:T(8,128)(2,1)S(1)}, u32[]{:S(2)}, u32[]{:S(2)}) collective-permute-start(bf16[128,256]{1,0:T(8,128)(2,1)S(1)} %collective-permute-done.refs_1_), channel_id=1, source_target_pairs={{0,4},{4,0},{8,12},{12,8},{16,20},{20,16},{24,28},{28,24},{1,5},{5... | collective-permute-start | bytes 196616 | tf_op jit(solution)/shard_map/ppermute | solution.py:144
  13.3 1.6 %collective-permute-start.7 = (bf16[512,256]{1,0:T(8,128)(2,1)S(1)}, bf16[512,256]{1,0:T(8,128)(2,1)S(1)}, u32[]{:S(2)}, u32[]{:S(2)}) collective-permute-start(bf16[512,256]{1,0:T(8,128)(2,1)S(1)} %get-tuple-element.25), channel_id=1, source_target_pairs={{0,4},{4,0},{8,12},{12,8},{16,20},{20,16},{24,28},{28,24},{1,5},{5... | collective-permute-start | bytes 786440 | tf_op jit(solution)/shard_map/ppermute | solution.py:144
  15.0 4.6 %collective-permute-start.8 = (bf16[128,256]{1,0:T(8,128)(2,1)S(1)}, bf16[128,256]{1,0:T(8,128)(2,1)S(1)}, u32[]{:S(2)}, u32[]{:S(2)}) collective-permute-start(bf16[128,256]{1,0:T(8,128)(2,1)S(1)} %get-tuple-element.28), channel_id=1, source_target_pairs={{0,8},{4,12},{8,0},{12,4},{16,24},{20,28},{24,16},{28,20},{1,9},{5... | collective-permute-start | bytes 196616 | tf_op jit(solution)/shard_map/ppermute | solution.py:144
  15.6 6.0 %collective-permute-start.10 = (bf16[128,256]{1,0:T(8,128)(2,1)S(1)}, bf16[128,256]{1,0:T(8,128)(2,1)S(1)}, u32[]{:S(2)}, u32[]{:S(2)}) collective-permute-start(bf16[128,256]{1,0:T(8,128)(2,1)S(1)} %get-tuple-element.29), channel_id=1, source_target_pairs={{0,24},{4,28},{8,16},{12,20},{16,8},{20,12},{24,0},{28,4},{1,25},{... | collective-permute-start | bytes 196616 | tf_op jit(solution)/shard_map/ppermute | solution.py:144
  18.0 4.6 %collective-permute-start.9 = (bf16[128,256]{1,0:T(8,128)(2,1)S(1)}, bf16[128,256]{1,0:T(8,128)(2,1)S(1)}, u32[]{:S(2)}, u32[]{:S(2)}) collective-permute-start(bf16[128,256]{1,0:T(8,128)(2,1)S(1)} %get-tuple-element.30), channel_id=1, source_target_pairs={{0,16},{4,20},{8,24},{12,28},{16,0},{20,4},{24,8},{28,12},{1,17},{... | collective-permute-start | bytes 196616 | tf_op jit(solution)/shard_map/ppermute | solution.py:144
  22.6 6.9 %collective-permute-start.13 = (bf16[128,256]{1,0:T(8,128)(2,1)S(1)}, bf16[128,256]{1,0:T(8,128)(2,1)S(1)}, u32[]{:S(2)}, u32[]{:S(2)}) collective-permute-start(bf16[128,256]{1,0:T(8,128)(2,1)S(1)} %fusion.2), channel_id=1, source_target_pairs={{0,3},{1,2},{2,1},{3,0},{4,7},{5,6},{6,5},{7,4},{8,11},{9,10},{10,... | collective-permute-start | bytes 196616 | tf_op jit(solution)/shard_map/ppermute | solution.py:144
  26.3 5.5 %collective-permute-start.12 = (bf16[128,256]{1,0:T(8,128)(2,1)S(1)}, bf16[128,256]{1,0:T(8,128)(2,1)S(1)}, u32[]{:S(2)}, u32[]{:S(2)}) collective-permute-start(bf16[128,256]{1,0:T(8,128)(2,1)S(1)} %fusion.2), channel_id=1, source_target_pairs={{0,2},{1,3},{2,0},{3,1},{4,6},{5,7},{6,4},{7,5},{8,10},{9,11},{10,... | collective-permute-start | bytes 196616 | tf_op jit(solution)/shard_map/ppermute | solution.py:144
  26.3 5.5 %collective-permute-start.11 = (bf16[128,256]{1,0:T(8,128)(2,1)S(1)}, bf16[128,256]{1,0:T(8,128)(2,1)S(1)}, u32[]{:S(2)}, u32[]{:S(2)}) collective-permute-start(bf16[128,256]{1,0:T(8,128)(2,1)S(1)} %fusion.2), channel_id=1, source_target_pairs={{0,1},{1,0},{2,3},{3,2},{4,5},{5,4},{6,7},{7,6},{8,9},{9,8},{10,11... | collective-permute-start | bytes 196616 | tf_op jit(solution)/shard_map/ppermute | solution.py:144

commit v3 on v1

v3 whole, which is shorter than its diff:
```python
import functools

import jax
import jax.numpy as jnp
from jax import lax
from jax.experimental import pallas as pl
from jax.experimental.pallas import tpu as pltpu
from jax.sharding import PartitionSpec as P


EPSILON = 1e-06
VMEM_LIMIT = 16 * 1024 * 1024


def contract(left, right, left_dim, right_dim):
    return lax.dot_general(
        left, right, (((left_dim,), (right_dim,)), ((), ())), preferred_element_type=jnp.float32
    )


def call(kernel, outs, *operands, space=pltpu.VMEM, scratch=()):
    return pl.pallas_call(
        kernel,
        out_shape=[pltpu.VMEM(shape, kind) for shape, kind in outs],
        in_specs=[pl.BlockSpec(memory_space=space)] * len(operands),
        out_specs=[pl.BlockSpec(memory_space=pltpu.VMEM)] * len(outs),
        scratch_shapes=scratch,
        compiler_params=pltpu.CompilerParams(vmem_limit_bytes=VMEM_LIMIT),
    )(*[pltpu.with_memory_space_constraint(x, space) for x in operands])


def run(copies, sems):
    copies = [
        pltpu.make_async_copy(source, target, sems.at[i])
        for i, (source, target) in enumerate(copies)
    ]
    for copy in copies:
        copy.start()
    for copy in copies:
        copy.wait()


def load_pair_kernel(key_hbm, value_hbm, pair_ref, sems):
    head_width = key_hbm.shape[1]
    run([(key_hbm, pair_ref.at[:, :head_width]), (value_hbm, pair_ref.at[:, head_width:])], sems)


def load_kernel(query_hbm, grad_hbm, stack_ref, grad_ref, sems):
    rows, head_width = query_hbm.shape[0], stack_ref.shape[1]
    heads = query_hbm.shape[1] // head_width
    copies = [(grad_hbm, grad_ref)]
    for h in range(heads):
        source = query_hbm.at[:, pl.ds(h * head_width, head_width)]
        copies.append((source, stack_ref.at[pl.ds(h * rows, rows), :]))
    run(copies, sems)
    for h in range(heads):
        turned = grad_ref[:, h * head_width : (h + 1) * head_width].T
        below = heads * rows + h * head_width
        stack_ref[below : below + head_width, :] = turned


def halves(refs):
    width = refs[0].shape[1] // 2
    return (
        jnp.concatenate([ref[:, :width] for ref in refs], axis=0),
        jnp.concatenate([ref[:, width:] for ref in refs], axis=0),
    )


def queries(own_ref, other_ref):
    count = own_ref.shape[0] // 2
    return jnp.concatenate([own_ref[:count, :], other_ref[:count, :]], axis=0)


def cotangents(own_ref, other_ref):
    width = own_ref.shape[1]
    count = own_ref.shape[0]
    tiles = [
        ref[at : at + width, :]
        for ref in (own_ref, other_ref)
        for at in range(count // 2, count, width)
    ]
    return jnp.concatenate(tiles, axis=1)


def forward_kernel(masks, *refs):
    slots, (own_ref, other_ref, score_ref, kept_ref, sent_ref) = refs[:-5], refs[-5:]
    rows = slots[0].shape[0]
    own = lax.axis_index("seq")
    query = queries(own_ref, other_ref)
    columns = query.shape[0] // 2
    keys, values = halves(slots)
    score = contract(keys, query, 1, 1)
    pieces = []
    for i, mask in enumerate(masks):
        piece = score[i * rows : (i + 1) * rows, :]
        if mask == 0:
            key_place = lax.broadcasted_iota(jnp.int32, (rows, columns), 0)
            query_place = lax.broadcasted_iota(jnp.int32, (rows, columns), 1) % rows
            here = jnp.where(key_place <= query_place, piece[:, :columns], 0.0)
            there = jnp.where(own < (own ^ 1), piece[:, columns:], 0.0)
            piece = jnp.concatenate([here, there], axis=1)
        else:
            piece = jnp.where((own ^ mask) < own, piece, 0.0)
        pieces.append(piece)
    score = jnp.concatenate(pieces, axis=0)
    score_ref[...] = score
    numerator = contract(values, (score * score).astype(jnp.bfloat16), 0, 0)
    kept_ref[...] = numerator
    sent_ref[:, :columns] = numerator[:, columns:].astype(jnp.bfloat16)
    sent_ref[:, columns:] = numerator[:, :columns].astype(jnp.bfloat16)


def backward_kernel(count, *refs):
    slots, refs = refs[:count], refs[count:]
    score_ref, kept_ref, came_ref, own_ref, other_ref, normed_ref, coefficient_ref = refs[:7]
    dkv_refs = refs[7:]
    rows, head_width = slots[0].shape[0], slots[0].shape[1] // 2
    numerator = kept_ref[...] + came_ref[...].astype(jnp.float32)
    root_mean = jnp.sqrt(jnp.mean(numerator * numerator, axis=0, keepdims=True) + EPSILON)
    normed = numerator / root_mean
    grad = cotangents(own_ref, other_ref).astype(jnp.float32)
    numer_grad = (
        (grad - normed * jnp.mean(grad * normed, axis=0, keepdims=True)) / root_mean
    ).astype(jnp.bfloat16)
    _, values = halves(slots)
    score = score_ref[...]
    coefficient = (2.0 * score * contract(values, numer_grad, 1, 0)).astype(jnp.bfloat16)
    weight = (score * score).astype(jnp.bfloat16)
    coefficient_ref[...] = coefficient
    normed_ref[...] = normed[:, : normed_ref.shape[1]].astype(jnp.bfloat16)
    dkey = contract(coefficient, queries(own_ref, other_ref), 1, 0)
    dvalue = contract(weight, numer_grad, 1, 1)
    for i, dkv_ref in enumerate(dkv_refs):
        span = slice(i * rows, (i + 1) * rows)
        dkv_ref[:, :head_width] = dkey[span, :].astype(dkv_ref.dtype)
        dkv_ref[:, head_width:] = dvalue[span, :].astype(dkv_ref.dtype)


def query_kernel(*refs):
    slots, (normed_ref, coefficient_ref, out_ref, kept_ref, sent_ref) = refs[:-5], refs[-5:]
    rows, head_width = slots[0].shape[0], slots[0].shape[1] // 2
    keys, _ = halves(slots)
    dquery = contract(keys, coefficient_ref[...], 0, 0)
    columns = kept_ref.shape[1]
    kept_ref[...] = dquery[:, :columns]
    sent_ref[...] = dquery[:, columns:].astype(jnp.bfloat16)
    for h in range(columns // rows):
        out_ref[:, h * head_width : (h + 1) * head_width] = normed_ref[
            :, h * rows : (h + 1) * rows
        ].T


def query_sum_kernel(kept_ref, came_ref, out_ref):
    rows, head_width = out_ref.shape[0], kept_ref.shape[0]
    total = (kept_ref[...] + came_ref[...].astype(jnp.float32)).astype(jnp.bfloat16)
    for h in range(out_ref.shape[1] // head_width):
        out_ref[:, h * head_width : (h + 1) * head_width] = total[:, h * rows : (h + 1) * rows].T


def partner(array, axis, mask):
    return lax.ppermute(array, axis, [(i, i ^ mask) for i in range(lax.axis_size(axis))])


def shifted(array, axis, step):
    size = lax.axis_size(axis)
    return lax.ppermute(array, axis, [(i, (i + step) % size) for i in range(size)])


def local(query_rows, key_rows, value_rows, out_grad):
    rows, head_width = key_rows.shape
    blocks, head_axis = lax.axis_size("seq"), lax.axis_size("head")
    heads = query_rows.shape[1] // head_width
    columns = heads * rows
    masks = tuple(range(0, blocks, 2))
    half = rows * len(masks)
    low, full = jnp.bfloat16, jnp.float32
    (pair,) = call(
        load_pair_kernel,
        [((rows, 2 * head_width), low)],
        key_rows,
        value_rows,
        space=pltpu.HBM,
        scratch=[pltpu.SemaphoreType.DMA((2,))],
    )
    slots = [pair] + [partner(pair, "seq", m) for m in masks[1:]]
    (own,) = call(
        load_kernel,
        [((heads * (rows + head_width), head_width), low)],
        query_rows,
        out_grad,
        space=pltpu.HBM,
        scratch=[pltpu.VMEM(out_grad.shape, low), pltpu.SemaphoreType.DMA((1 + heads,))],
    )
    other = partner(own, "seq", 1)
    score, kept, sent = call(
        functools.partial(forward_kernel, masks),
        [
            ((half, 2 * columns), full),
            ((head_width, 2 * columns), full),
            ((head_width, 2 * columns), low),
        ],
        *slots,
        own,
        other,
    )
    came = partner(sent, "seq", 1)
    normed, coefficient, summed, *away = call(
        functools.partial(backward_kernel, len(slots)),
        [((head_width, columns), low), ((half, 2 * columns), low), ((rows, 2 * head_width), full)]
        + [((rows, 2 * head_width), low)] * (len(masks) - 1),
        *slots,
        score,
        kept,
        came,
        own,
        other,
    )
    for mask, piece in zip(masks[1:], away):
        summed = summed + partner(piece, "seq", mask).astype(full)
    attended, dquery, dquery_other = call(
        query_kernel,
        [(query_rows.shape, low), ((head_width, columns), full), ((head_width, columns), low)],
        *slots,
        normed,
        coefficient,
    )
    (query_grad,) = call(
        query_sum_kernel, [(query_rows.shape, low)], dquery, partner(dquery_other, "seq", 1)
    )
    sent = summed.astype(low)
    for step in range(1, head_axis):
        summed = summed + shifted(sent, "head", step).astype(full)
    summed = summed.astype(low)
    return (attended, query_grad, summed[:, :head_width], summed[:, head_width:])


def solution(mesh):
    placed = (P("seq", "head"), P("seq", None), P("seq", None), P("seq", "head"))

    return jax.shard_map(
        local,
        mesh=mesh,
        in_specs=placed,
        out_specs=(P("seq", "head"), P("seq", "head"), P("seq", None), P("seq", None)),
        check_vma=False,
    )
```

time: 51.4 us -> 33.4 us (0.65)
  blocking collectives: 35.1 us -> 0 us
  waiting for transfers between devices: 5.05 us -> 13.4 us
  starting transfers between devices: 4.67 us -> 13 us
  local copies, waits for them, and re-layouts: 0.64 us -> 1.95 us
  Pallas kernels: 4.8 us -> 4.04 us
    all_gather x2 -> x0, blocking collectives: 22 us -> none  [the longest x1 12.6 us: local(): keys = lax.all_gather(key_rows, 'seq', axis=0, tiled=True)]
    all_to_all x1 -> x0, blocking collectives: 13.1 us -> none  [local(): lax.all_to_all(partial.reshape(blocks, rows, 2 * head_width), 'seq', 0, 0)]
    ppermute x3 -> x12, waiting for transfers between devices: 5.05 us -> 13.4 us  [the longest x9 9.38 us: partner(): lax.ppermute(array, axis, [(i, i ^ mask) for i in range(lax.axis_size(axi...]
    ppermute x3 -> x12, starting transfers between devices: 4.67 us -> 13 us  [the longest x9 8.34 us: partner(): lax.ppermute(array, axis, [(i, i ^ mask) for i in range(lax.axis_size(axi...]
    unnamed x2, local copies, waits for them, and re-layouts: 0.01 us -> 1.32 us
    pallas_call x1 -> x6, Pallas kernels: 4.8 us -> 4.04 us  [call(): pl.pallas_call(kernel, out_shape=[pltpu.VMEM(shape, kind) for shape, kind...]
  transfers between devices with their start and end apart: 3 -> 12, of which waited for: 3 -> 9; matrix products, arithmetic and copies ran while one was open for 0% -> 4% of each run, Pallas kernels for 0% -> 3%
where the time goes in v3:
time: 33.4 us; the launch traced here: 33.2 us
  waiting for transfers between devices  13.4 us (40%)
  starting transfers between devices  13 us (39%)
  Pallas kernels  4.04 us (12%)
  local copies, waits for them, and re-layouts  1.95 us (6%)
  between operations  0.7 us (2%)
    ppermute x9, waiting for transfers between devices, partner(): lax.ppermute(array, axis, [(i, i ^ mask) for i in range(lax.axis_size(axi...  9.38 us
    ppermute x9, starting transfers between devices, partner(): lax.ppermute(array, axis, [(i, i ^ mask) for i in range(lax.axis_size(axi...  8.34 us
    ppermute x3, starting transfers between devices, shifted(): lax.ppermute(array, axis, [(i, (i + step) % size) for i in range(size)])  4.67 us
    ppermute x3, waiting for transfers between devices, shifted(): lax.ppermute(array, axis, [(i, (i + step) % size) for i in range(size)])  4.05 us
    pallas_call x6, Pallas kernels, call(): pl.pallas_call(kernel, out_shape=[pltpu.VMEM(shape, kind) for shape, kind...  4.04 us
    unnamed x2, local copies, waits for them, and re-layouts  1.32 us
  transfers between devices with their start and end apart: 12, of which 9 were waited for; matrix products, arithmetic and copies ran while one was open for 4% of the time, Pallas kernels for 3%

profile of v3, /device:TPU:0, one launch (start us, length us, event | category | flops | bytes accessed | tf_op | source)
XLA Modules:
  0.0 33.2 jit_solution(9584264586160390242)
XLA Ops:
  0.6 1.0 %shard_map.76.refs_4_.refs_7_ = bf16[1024,128]{1,0:T(8,128)(2,1)S(1)} custom-call(bf16[128,512]{1,0:T(8,128)(2,1)} %query_hbm.1, bf16[128,512]{1,0:T(8,128)(2,1)} %grad_hbm.1), custom_call_target="tpu_custom_call" | custom-call | tf_op jit(solution)/shard_map/pallas_call | solution.py:22
  1.7 0.6 %collective-permute-start.3 = (bf16[1024,128]{1,0:T(8,128)(2,1)S(1)}, bf16[1024,128]{1,0:T(8,128)(2,1)S(1)}, u32[]{:S(2)}, u32[]{:S(2)}) collective-permute-start(bf16[1024,128]{1,0:T(8,128)(2,1)S(1)} %shard_map.76.refs_4_.refs_7_), channel_id=1, source_target_pairs={{0,4},{4,0},{8,12},{12,8},{16,20},{20,16},{24,28},{28,24},{1,5},{5... | collective-permute-start | bytes 786440 | tf_op jit(solution)/shard_map/ppermute | solution.py:162
  2.2 0.8 %shard_map.75.refs_0_ = bf16[128,256]{1,0:T(8,128)(2,1)S(1)} custom-call(bf16[128,128]{1,0:T(8,128)(2,1)} %key_hbm.1, bf16[128,128]{1,0:T(8,128)(2,1)} %value_hbm.1), custom_call_target="tpu_custom_call" | custom-call | tf_op jit(solution)/shard_map/pallas_call | solution.py:22
  3.0 3.5 %collective-permute-start.2 = (bf16[128,256]{1,0:T(8,128)(2,1)S(1)}, bf16[128,256]{1,0:T(8,128)(2,1)S(1)}, u32[]{:S(2)}, u32[]{:S(2)}) collective-permute-start(bf16[128,256]{1,0:T(8,128)(2,1)S(1)} %shard_map.75.refs_0_), channel_id=1, source_target_pairs={{0,24},{4,28},{8,16},{12,20},{16,8},{20,12},{24,0},{28,4},{1,25},{... | collective-permute-start | bytes 196616 | tf_op jit(solution)/shard_map/ppermute | solution.py:162
  6.6 0.5 %collective-permute-start.1 = (bf16[128,256]{1,0:T(8,128)(2,1)S(1)}, bf16[128,256]{1,0:T(8,128)(2,1)S(1)}, u32[]{:S(2)}, u32[]{:S(2)}) collective-permute-start(bf16[128,256]{1,0:T(8,128)(2,1)S(1)} %shard_map.75.refs_0_), channel_id=1, source_target_pairs={{0,16},{4,20},{8,24},{12,28},{16,0},{20,4},{24,8},{28,12},{1,17},{... | collective-permute-start | bytes 196616 | tf_op jit(solution)/shard_map/ppermute | solution.py:162
  7.1 0.1 collective-permute-start
  7.2 2.1 %collective-permute-done.2.refs_3_ = bf16[128,256]{1,0:T(8,128)(2,1)S(1)} collective-permute-done((bf16[128,256]{1,0:T(8,128)(2,1)S(1)}, bf16[128,256]{1,0:T(8,128)(2,1)S(1)}, u32[]{:S(2)}, u32[]{:S(2)}) %collective-permute-start.2) | collective-permute-done | bytes 65568 | tf_op jit(solution)/shard_map/ppermute | solution.py:162
  9.3 1.5 %collective-permute-done.1.refs_2_ = bf16[128,256]{1,0:T(8,128)(2,1)S(1)} collective-permute-done((bf16[128,256]{1,0:T(8,128)(2,1)S(1)}, bf16[128,256]{1,0:T(8,128)(2,1)S(1)}, u32[]{:S(2)}, u32[]{:S(2)}) %collective-permute-start.1) | collective-permute-done | bytes 65568 | tf_op jit(solution)/shard_map/ppermute | solution.py:162
  10.8 0.5 %collective-permute-done.refs_1_ = bf16[128,256]{1,0:T(8,128)(2,1)S(1)} collective-permute-done((bf16[128,256]{1,0:T(8,128)(2,1)S(1)}, bf16[128,256]{1,0:T(8,128)(2,1)S(1)}, u32[]{:S(2)}, u32[]{:S(2)}) %collective-permute-start) | collective-permute-done | bytes 65568 | tf_op jit(solution)/shard_map/ppermute | solution.py:162
  11.3 0.0 collective-permute-done.3.refs_5_.refs_8_
  11.3 0.6 %shard_map.77 = (f32[512,1024]{1,0:T(8,128)S(1)}, f32[128,1024]{1,0:T(8,128)S(1)}, bf16[128,1024]{1,0:T(8,128)(2,1)S(1)}) custom-call(bf16[128,256]{1,0:T(8,128)(2,1)S(1)} %shard_map.75.refs_0_, bf16[128,256]{1,0:T(8,128)(2,1)S(1)} %collective-permute-done.refs_1_, bf16[128,256]{1,0:T(8,128)(2,1)S(1)} %collective-permute-done.1.refs_2_, ...), custom_call_target="tpu_custom_call" | custom-call | tf_op jit(solution)/shard_map/pallas_call | solution.py:22
  11.9 0.1 collective-permute-start.4
  12.0 1.5 %collective-permute-done.4.refs_6_ = bf16[128,1024]{1,0:T(8,128)(2,1)S(1)} collective-permute-done((bf16[128,1024]{1,0:T(8,128)(2,1)S(1)}, bf16[128,1024]{1,0:T(8,128)(2,1)S(1)}, u32[]{:S(2)}, u32[]{:S(2)}) %collective-permute-start.4) | collective-permute-done | bytes 262176 | tf_op jit(solution)/shard_map/ppermute | solution.py:162
  13.5 1.2 %shard_map.78 = (bf16[128,512]{1,0:T(8,128)(2,1)S(1)}, bf16[512,1024]{1,0:T(8,128)(2,1)S(1)}, f32[128,256]{1,0:T(8,128)S(1)}, bf16[128,256]{1,0:T(8,128)(2,1)S(1...) custom-call(bf16[128,256]{1,0:T(8,128)(2,1)S(1)} %shard_map.75.refs_0_, ...), custom_call_target="tpu_custom_call" | custom-call | tf_op jit(solution)/shard_map/pallas_call | solution.py:22
  14.7 1.2 %collective-permute-start.6 = (bf16[128,256]{1,0:T(8,128)(2,1)S(1)}, bf16[128,256]{1,0:T(8,128)(2,1)S(1)}, u32[]{:S(2)}, u32[]{:S(2)}) collective-permute-start(bf16[128,256]{1,0:T(8,128)(2,1)S(1)} %get-tuple-element.25), channel_id=1, source_target_pairs={{0,8},{4,12},{8,0},{12,4},{16,24},{20,28},{24,16},{28,20},{1,9},{5... | collective-permute-start | bytes 196616 | tf_op jit(solution)/shard_map/ppermute | solution.py:162
  15.9 0.9 %collective-permute-start.7 = (bf16[128,256]{1,0:T(8,128)(2,1)S(1)}, bf16[128,256]{1,0:T(8,128)(2,1)S(1)}, u32[]{:S(2)}, u32[]{:S(2)}) collective-permute-start(bf16[128,256]{1,0:T(8,128)(2,1)S(1)} %get-tuple-element.26), channel_id=1, source_target_pairs={{0,16},{4,20},{8,24},{12,28},{16,0},{20,4},{24,8},{28,12},{1,17},{... | collective-permute-start | bytes 196616 | tf_op jit(solution)/shard_map/ppermute | solution.py:162
  16.8 1.4 %collective-permute-start.8 = (bf16[128,256]{1,0:T(8,128)(2,1)S(1)}, bf16[128,256]{1,0:T(8,128)(2,1)S(1)}, u32[]{:S(2)}, u32[]{:S(2)}) collective-permute-start(bf16[128,256]{1,0:T(8,128)(2,1)S(1)} %get-tuple-element.27), channel_id=1, source_target_pairs={{0,24},{4,28},{8,16},{12,20},{16,8},{20,12},{24,0},{28,4},{1,25},{... | collective-permute-start | bytes 196616 | tf_op jit(solution)/shard_map/ppermute | solution.py:162
  18.3 0.8 %collective-permute-done.6 = bf16[128,256]{1,0:T(8,128)(2,1)S(1)} collective-permute-done((bf16[128,256]{1,0:T(8,128)(2,1)S(1)}, bf16[128,256]{1,0:T(8,128)(2,1)S(1)}, u32[]{:S(2)}, u32[]{:S(2)}) %collective-permute-start.6) | collective-permute-done | bytes 65568 | tf_op jit(solution)/shard_map/ppermute | solution.py:162
  19.1 1.8 %collective-permute-done.7 = bf16[128,256]{1,0:T(8,128)(2,1)S(1)} collective-permute-done((bf16[128,256]{1,0:T(8,128)(2,1)S(1)}, bf16[128,256]{1,0:T(8,128)(2,1)S(1)}, u32[]{:S(2)}, u32[]{:S(2)}) %collective-permute-start.7) | collective-permute-done | bytes 65568 | tf_op jit(solution)/shard_map/ppermute | solution.py:162
  20.9 1.1 %collective-permute-done.8 = bf16[128,256]{1,0:T(8,128)(2,1)S(1)} collective-permute-done((bf16[128,256]{1,0:T(8,128)(2,1)S(1)}, bf16[128,256]{1,0:T(8,128)(2,1)S(1)}, u32[]{:S(2)}, u32[]{:S(2)}) %collective-permute-start.8) | collective-permute-done | bytes 65568 | tf_op jit(solution)/shard_map/ppermute | solution.py:162
  22.0 3.7 %collective-permute-start.11 = (bf16[128,256]{1,0:T(8,128)(2,1)S(1)}, bf16[128,256]{1,0:T(8,128)(2,1)S(1)}, u32[]{:S(2)}, u32[]{:S(2)}) collective-permute-start(bf16[128,256]{1,0:T(8,128)(2,1)S(1)} %fusion), channel_id=1, source_target_pairs={{0,3},{1,0},{2,1},{3,2},{4,7},{5,4},{6,5},{7,6},{8,11},{9,8},{10,9... | collective-permute-start | bytes 196616 | tf_op jit(solution)/shard_map/ppermute | solution.py:167
  25.7 0.0 collective-permute-start.10
  25.7 1.0 %collective-permute-start.9 = (bf16[128,256]{1,0:T(8,128)(2,1)S(1)}, bf16[128,256]{1,0:T(8,128)(2,1)S(1)}, u32[]{:S(2)}, u32[]{:S(2)}) collective-permute-start(bf16[128,256]{1,0:T(8,128)(2,1)S(1)} %fusion), channel_id=1, source_target_pairs={{0,1},{1,2},{2,3},{3,0},{4,5},{5,6},{6,7},{7,4},{8,9},{9,10},{10,1... | collective-permute-start | bytes 196616 | tf_op jit(solution)/shard_map/ppermute | solution.py:167
  26.7 0.3 shard_map.79
  27.1 0.7 %copy.8 = bf16[128,512]{1,0:T(8,128)(2,1)} copy(bf16[128,512]{1,0:T(8,128)(2,1)S(1)} %get-tuple-element.30) | data formatting | bytes 262144
  27.7 0.0 collective-permute-start.5
  27.7 0.0 collective-permute-done.11
  27.7 3.1 %collective-permute-done.10 = bf16[128,256]{1,0:T(8,128)(2,1)S(1)} collective-permute-done((bf16[128,256]{1,0:T(8,128)(2,1)S(1)}, bf16[128,256]{1,0:T(8,128)(2,1)S(1)}, u32[]{:S(2)}, u32[]{:S(2)}) %collective-permute-start.10) | collective-permute-done | bytes 65568 | tf_op jit(solution)/shard_map/ppermute | solution.py:167
  30.9 0.9 %collective-permute-done.9 = bf16[128,256]{1,0:T(8,128)(2,1)S(1)} collective-permute-done((bf16[128,256]{1,0:T(8,128)(2,1)S(1)}, bf16[128,256]{1,0:T(8,128)(2,1)S(1)}, u32[]{:S(2)}, u32[]{:S(2)}) %collective-permute-start.9) | collective-permute-done | bytes 65568 | tf_op jit(solution)/shard_map/ppermute | solution.py:167
  31.8 0.1 add_convert_fusion
  31.8 0.6 %fusion.1 = (bf16[128,128]{1,0:T(8,128)(2,1)}, bf16[128,128]{1,0:T(8,128)(2,1)}) fusion(bf16[128,256]{1,0:T(8,128)(2,1)S(1)} %add_convert_fusion), kind=kLoop, calls=%fused_computation.3 | loop fusion | bytes 131072 | tf_op jit(solution)/shard_map/slice | solution.py:235
  32.5 0.0 collective-permute-done.5.came_ref
  32.5 0.1 shard_map.80
  32.6 0.7 %copy.9 = bf16[128,512]{1,0:T(8,128)(2,1)} copy(bf16[128,512]{1,0:T(8,128)(2,1)S(1)} %shard_map.80) | data formatting | bytes 262144
  (1 shorter events, 0.0 us)
Async XLA Ops:
  1.7 9.6 %collective-permute-start.3 = (bf16[1024,128]{1,0:T(8,128)(2,1)S(1)}, bf16[1024,128]{1,0:T(8,128)(2,1)S(1)}, u32[]{:S(2)}, u32[]{:S(2)}) collective-permute-start(bf16[1024,128]{1,0:T(8,128)(2,1)S(1)} %shard_map.76.refs_4_.refs_7_), channel_id=1, source_target_pairs={{0,4},{4,0},{8,12},{12,8},{16,20},{20,16},{24,28},{28,24},{1,5},{5... | collective-permute-start | bytes 786440 | tf_op jit(solution)/shard_map/ppermute | solution.py:162
  3.0 6.3 %collective-permute-start.2 = (bf16[128,256]{1,0:T(8,128)(2,1)S(1)}, bf16[128,256]{1,0:T(8,128)(2,1)S(1)}, u32[]{:S(2)}, u32[]{:S(2)}) collective-permute-start(bf16[128,256]{1,0:T(8,128)(2,1)S(1)} %shard_map.75.refs_0_), channel_id=1, source_target_pairs={{0,24},{4,28},{8,16},{12,20},{16,8},{20,12},{24,0},{28,4},{1,25},{... | collective-permute-start | bytes 196616 | tf_op jit(solution)/shard_map/ppermute | solution.py:162
  6.6 4.3 %collective-permute-start.1 = (bf16[128,256]{1,0:T(8,128)(2,1)S(1)}, bf16[128,256]{1,0:T(8,128)(2,1)S(1)}, u32[]{:S(2)}, u32[]{:S(2)}) collective-permute-start(bf16[128,256]{1,0:T(8,128)(2,1)S(1)} %shard_map.75.refs_0_), channel_id=1, source_target_pairs={{0,16},{4,20},{8,24},{12,28},{16,0},{20,4},{24,8},{28,12},{1,17},{... | collective-permute-start | bytes 196616 | tf_op jit(solution)/shard_map/ppermute | solution.py:162
  7.1 4.3 %collective-permute-start = (bf16[128,256]{1,0:T(8,128)(2,1)S(1)}, bf16[128,256]{1,0:T(8,128)(2,1)S(1)}, u32[]{:S(2)}, u32[]{:S(2)}) collective-permute-start(bf16[128,256]{1,0:T(8,128)(2,1)S(1)} %shard_map.75.refs_0_), channel_id=1, source_target_pairs={{0,8},{4,12},{8,0},{12,4},{16,24},{20,28},{24,16},{28,20},{1,9},{5... | collective-permute-start | bytes 196616 | tf_op jit(solution)/shard_map/ppermute | solution.py:162
  11.9 1.6 %collective-permute-start.4 = (bf16[128,1024]{1,0:T(8,128)(2,1)S(1)}, bf16[128,1024]{1,0:T(8,128)(2,1)S(1)}, u32[]{:S(2)}, u32[]{:S(2)}) collective-permute-start(bf16[128,1024]{1,0:T(8,128)(2,1)S(1)} %get-tuple-element.18), channel_id=1, source_target_pairs={{0,4},{4,0},{8,12},{12,8},{16,20},{20,16},{24,28},{28,24},{1,5},{5... | collective-permute-start | bytes 786440 | tf_op jit(solution)/shard_map/ppermute | solution.py:162
  14.7 4.3 %collective-permute-start.6 = (bf16[128,256]{1,0:T(8,128)(2,1)S(1)}, bf16[128,256]{1,0:T(8,128)(2,1)S(1)}, u32[]{:S(2)}, u32[]{:S(2)}) collective-permute-start(bf16[128,256]{1,0:T(8,128)(2,1)S(1)} %get-tuple-element.25), channel_id=1, source_target_pairs={{0,8},{4,12},{8,0},{12,4},{16,24},{20,28},{24,16},{28,20},{1,9},{5... | collective-permute-start | bytes 196616 | tf_op jit(solution)/shard_map/ppermute | solution.py:162
  15.9 5.0 %collective-permute-start.7 = (bf16[128,256]{1,0:T(8,128)(2,1)S(1)}, bf16[128,256]{1,0:T(8,128)(2,1)S(1)}, u32[]{:S(2)}, u32[]{:S(2)}) collective-permute-start(bf16[128,256]{1,0:T(8,128)(2,1)S(1)} %get-tuple-element.26), channel_id=1, source_target_pairs={{0,16},{4,20},{8,24},{12,28},{16,0},{20,4},{24,8},{28,12},{1,17},{... | collective-permute-start | bytes 196616 | tf_op jit(solution)/shard_map/ppermute | solution.py:162
  16.8 5.2 %collective-permute-start.8 = (bf16[128,256]{1,0:T(8,128)(2,1)S(1)}, bf16[128,256]{1,0:T(8,128)(2,1)S(1)}, u32[]{:S(2)}, u32[]{:S(2)}) collective-permute-start(bf16[128,256]{1,0:T(8,128)(2,1)S(1)} %get-tuple-element.27), channel_id=1, source_target_pairs={{0,24},{4,28},{8,16},{12,20},{16,8},{20,12},{24,0},{28,4},{1,25},{... | collective-permute-start | bytes 196616 | tf_op jit(solution)/shard_map/ppermute | solution.py:162
  22.0 5.7 %collective-permute-start.11 = (bf16[128,256]{1,0:T(8,128)(2,1)S(1)}, bf16[128,256]{1,0:T(8,128)(2,1)S(1)}, u32[]{:S(2)}, u32[]{:S(2)}) collective-permute-start(bf16[128,256]{1,0:T(8,128)(2,1)S(1)} %fusion), channel_id=1, source_target_pairs={{0,3},{1,0},{2,1},{3,2},{4,7},{5,4},{6,5},{7,6},{8,11},{9,8},{10,9... | collective-permute-start | bytes 196616 | tf_op jit(solution)/shard_map/ppermute | solution.py:167
  25.7 5.2 %collective-permute-start.10 = (bf16[128,256]{1,0:T(8,128)(2,1)S(1)}, bf16[128,256]{1,0:T(8,128)(2,1)S(1)}, u32[]{:S(2)}, u32[]{:S(2)}) collective-permute-start(bf16[128,256]{1,0:T(8,128)(2,1)S(1)} %fusion), channel_id=1, source_target_pairs={{0,2},{1,3},{2,0},{3,1},{4,6},{5,7},{6,4},{7,5},{8,10},{9,11},{10,... | collective-permute-start | bytes 196616 | tf_op jit(solution)/shard_map/ppermute | solution.py:167
  25.7 6.1 %collective-permute-start.9 = (bf16[128,256]{1,0:T(8,128)(2,1)S(1)}, bf16[128,256]{1,0:T(8,128)(2,1)S(1)}, u32[]{:S(2)}, u32[]{:S(2)}) collective-permute-start(bf16[128,256]{1,0:T(8,128)(2,1)S(1)} %fusion), channel_id=1, source_target_pairs={{0,1},{1,2},{2,3},{3,0},{4,5},{5,6},{6,7},{7,4},{8,9},{9,10},{10,1... | collective-permute-start | bytes 196616 | tf_op jit(solution)/shard_map/ppermute | solution.py:167
  27.7 4.8 %collective-permute-start.5 = (bf16[128,512]{1,0:T(8,128)(2,1)S(1)}, bf16[128,512]{1,0:T(8,128)(2,1)S(1)}, u32[]{:S(2)}, u32[]{:S(2)}) collective-permute-start(bf16[128,512]{1,0:T(8,128)(2,1)S(1)} %get-tuple-element.23), channel_id=1, source_target_pairs={{0,4},{4,0},{8,12},{12,8},{16,20},{20,16},{24,28},{28,24},{1,5},{5... | collective-permute-start | bytes 393224 | tf_op jit(solution)/shard_map/ppermute | solution.py:162

commit v4 on v3

--- a/solution.py
+++ b/solution.py
@@ -84,64 +84,82 @@
 
 
 def forward_kernel(masks, *refs):
-    slots, (own_ref, other_ref, score_ref, kept_ref, sent_ref) = refs[:-5], refs[-5:]
+    slots, refs = refs[: len(masks)], refs[len(masks) :]
+    own_ref, other_ref, score_ref, weight_ref, kept_ref, sent_ref = refs
     rows = slots[0].shape[0]
     own = lax.axis_index("seq")
     query = queries(own_ref, other_ref)
     columns = query.shape[0] // 2
     keys, values = halves(slots)
-    score = contract(keys, query, 1, 1)
-    pieces = []
-    for i, mask in enumerate(masks):
-        piece = score[i * rows : (i + 1) * rows, :]
-        if mask == 0:
-            key_place = lax.broadcasted_iota(jnp.int32, (rows, columns), 0)
-            query_place = lax.broadcasted_iota(jnp.int32, (rows, columns), 1) % rows
-            here = jnp.where(key_place <= query_place, piece[:, :columns], 0.0)
-            there = jnp.where(own < (own ^ 1), piece[:, columns:], 0.0)
-            piece = jnp.concatenate([here, there], axis=1)
-        else:
-            piece = jnp.where((own ^ mask) < own, piece, 0.0)
-        pieces.append(piece)
-    score = jnp.concatenate(pieces, axis=0)
+    earlier = [
+        jnp.where((own ^ mask) < own, keys[i * rows : (i + 1) * rows, :], 0.0).astype(keys.dtype)
+        for i, mask in enumerate(masks)
+        if mask
+    ]
+    score = contract(jnp.concatenate([keys[:rows, :], *earlier], axis=0), query, 1, 1)
+    key_place = lax.broadcasted_iota(jnp.int32, (rows, columns), 0)
+    query_place = lax.broadcasted_iota(jnp.int32, (rows, columns), 1) % rows
+    here = jnp.where(key_place <= query_place, score[:rows, :columns], 0.0)
+    there = jnp.where(own < (own ^ 1), score[:rows, columns:], 0.0)
+    score = jnp.concatenate([jnp.concatenate([here, there], axis=1), score[rows:, :]], axis=0)
+    weight = (score * score).astype(jnp.bfloat16)
     score_ref[...] = score
-    numerator = contract(values, (score * score).astype(jnp.bfloat16), 0, 0)
+    weight_ref[...] = weight
+    numerator = contract(values, weight, 0, 0)
     kept_ref[...] = numerator
     sent_ref[:, :columns] = numerator[:, columns:].astype(jnp.bfloat16)
     sent_ref[:, columns:] = numerator[:, :columns].astype(jnp.bfloat16)
 
 
-def backward_kernel(count, *refs):
+def key_side(values, score, weight, query, numer_grad):
+    coefficient = (score * contract(values, numer_grad, 1, 0)).astype(jnp.bfloat16)
+    dkey = 2.0 * contract(coefficient, query, 1, 0)
+    return coefficient, jnp.concatenate([dkey, contract(weight, numer_grad, 1, 1)], axis=1)
+
+
+def away_kernel(count, *refs):
     slots, refs = refs[:count], refs[count:]
-    score_ref, kept_ref, came_ref, own_ref, other_ref, normed_ref, coefficient_ref = refs[:7]
-    dkv_refs = refs[7:]
-    rows, head_width = slots[0].shape[0], slots[0].shape[1] // 2
+    score_ref, weight_ref, kept_ref, came_ref, own_ref, other_ref = refs[:6]
+    normed_ref, numer_ref, coefficient_ref = refs[6:9]
+    rows = slots[0].shape[0]
     numerator = kept_ref[...] + came_ref[...].astype(jnp.float32)
-    root_mean = jnp.sqrt(jnp.mean(numerator * numerator, axis=0, keepdims=True) + EPSILON)
-    normed = numerator / root_mean
+    inverse = 1.0 / jnp.sqrt(jnp.mean(numerator * numerator, axis=0, keepdims=True) + EPSILON)
+    normed = numerator * inverse
     grad = cotangents(own_ref, other_ref).astype(jnp.float32)
     numer_grad = (
-        (grad - normed * jnp.mean(grad * normed, axis=0, keepdims=True)) / root_mean
+        (grad - normed * jnp.mean(grad * normed, axis=0, keepdims=True)) * inverse
     ).astype(jnp.bfloat16)
     _, values = halves(slots)
-    score = score_ref[...]
-    coefficient = (2.0 * score * contract(values, numer_grad, 1, 0)).astype(jnp.bfloat16)
-    weight = (score * score).astype(jnp.bfloat16)
+    coefficient, dkv = key_side(
+        values,
+        score_ref[rows:, :],
+        weight_ref[rows:, :],
+        queries(own_ref, other_ref),
+        numer_grad,
+    )
+    dkv = dkv.astype(jnp.bfloat16)
+    for i, dkv_ref in enumerate(refs[9:]):
+        dkv_ref[...] = dkv[i * rows : (i + 1) * rows, :]
     coefficient_ref[...] = coefficient
+    numer_ref[...] = numer_grad
     normed_ref[...] = normed[:, : normed_ref.shape[1]].astype(jnp.bfloat16)
-    dkey = contract(coefficient, queries(own_ref, other_ref), 1, 0)
-    dvalue = contract(weight, numer_grad, 1, 1)
-    for i, dkv_ref in enumerate(dkv_refs):
-        span = slice(i * rows, (i + 1) * rows)
-        dkv_ref[:, :head_width] = dkey[span, :].astype(dkv_ref.dtype)
-        dkv_ref[:, head_width:] = dvalue[span, :].astype(dkv_ref.dtype)
-
-
-def query_kernel(*refs):
-    slots, (normed_ref, coefficient_ref, out_ref, kept_ref, sent_ref) = refs[:-5], refs[-5:]
+
+
+def home_kernel(*refs):
+    slots, refs = refs[:-11], refs[-11:]
+    score_ref, weight_ref, own_ref, other_ref, numer_ref, coefficient_ref, normed_ref = refs[:7]
+    dkv_ref, out_ref, kept_ref, sent_ref = refs[7:]
     rows, head_width = slots[0].shape[0], slots[0].shape[1] // 2
-    keys, _ = halves(slots)
-    dquery = contract(keys, coefficient_ref[...], 0, 0)
+    keys, values = halves(slots)
+    coefficient, dkv_ref[...] = key_side(
+        values[:rows, :],
+        score_ref[:rows, :],
+        weight_ref[:rows, :],
+        queries(own_ref, other_ref),
+        numer_ref[...],
+    )
+    coefficient = jnp.concatenate([coefficient, coefficient_ref[...]], axis=0)
+    dquery = 2.0 * contract(keys, coefficient, 0, 0)
     columns = kept_ref.shape[1]
     kept_ref[...] = dquery[:, :columns]
     sent_ref[...] = dquery[:, columns:].astype(jnp.bfloat16)
@@ -193,10 +211,11 @@
         scratch=[pltpu.VMEM(out_grad.shape, low), pltpu.SemaphoreType.DMA((1 + heads,))],
     )
     other = partner(own, "seq", 1)
-    score, kept, sent = call(
+    score, weight, kept, sent = call(
         functools.partial(forward_kernel, masks),
         [
             ((half, 2 * columns), full),
+            ((half, 2 * columns), low),
             ((head_width, 2 * columns), full),
             ((head_width, 2 * columns), low),
         ],
@@ -205,26 +224,42 @@
         other,
     )
     came = partner(sent, "seq", 1)
-    normed, coefficient, summed, *away = call(
-        functools.partial(backward_kernel, len(slots)),
-        [((head_width, columns), low), ((half, 2 * columns), low), ((rows, 2 * head_width), full)]
+    normed, numer_grad, coefficient, *away = call(
+        functools.partial(away_kernel, len(slots) - 1),
+        [
+            ((head_width, columns), low),
+            ((head_width, 2 * columns), low),
+            ((half - rows, 2 * columns), low),
+        ]
         + [((rows, 2 * head_width), low)] * (len(masks) - 1),
-        *slots,
+        *slots[1:],
         score,
+        weight,
         kept,
         came,
         own,
         other,
     )
-    for mask, piece in zip(masks[1:], away):
-        summed = summed + partner(piece, "seq", mask).astype(full)
-    attended, dquery, dquery_other = call(
-        query_kernel,
-        [(query_rows.shape, low), ((head_width, columns), full), ((head_width, columns), low)],
+    arrived = [partner(piece, "seq", m) for m, piece in zip(masks[1:], away)]
+    summed, attended, dquery, dquery_other = call(
+        home_kernel,
+        [
+            ((rows, 2 * head_width), full),
+            (query_rows.shape, low),
+            ((head_width, columns), full),
+            ((head_width, columns), low),
+        ],
         *slots,
+        score,
+        weight,
+        own,
+        other,
+        numer_grad,
+        coefficient,
         normed,
-        coefficient,
-    )
+    )
+    for piece in arrived:
+        summed = summed + piece.astype(full)
     (query_grad,) = call(
         query_sum_kernel, [(query_rows.shape, low)], dquery, partner(dquery_other, "seq", 1)
     )

time: 33.4 us -> 33.2 us (level)
    ppermute x9, waiting for transfers between devices: 9.38 us -> 8.81 us  [partner(): lax.ppermute(array, axis, [(i, i ^ mask) for i in range(lax.axis_size(axi...]
    ppermute x3, waiting for transfers between devices: 4.05 us -> 4.39 us  [shifted(): lax.ppermute(array, axis, [(i, (i + step) % size) for i in range(size)])]
  transfers between devices with their start and end apart: 12 -> 12, of which waited for: 9 -> 10; matrix products, arithmetic and copies ran while one was open for 4% -> 4% of each run, Pallas kernels for 3% -> 4%
where the time goes in v4:
time: 33.2 us; the launch traced here: 33 us
  waiting for transfers between devices  13.2 us (40%)
  starting transfers between devices  13 us (39%)
  Pallas kernels  4.03 us (12%)
  local copies, waits for them, and re-layouts  1.94 us (6%)
  between operations  0.7 us (2%)
    ppermute x9, waiting for transfers between devices, partner(): lax.ppermute(array, axis, [(i, i ^ mask) for i in range(lax.axis_size(axi...  8.81 us
    ppermute x9, starting transfers between devices, partner(): lax.ppermute(array, axis, [(i, i ^ mask) for i in range(lax.axis_size(axi...  8.34 us
    ppermute x3, starting transfers between devices, shifted(): lax.ppermute(array, axis, [(i, (i + step) % size) for i in range(size)])  4.67 us
    ppermute x3, waiting for transfers between devices, shifted(): lax.ppermute(array, axis, [(i, (i + step) % size) for i in range(size)])  4.39 us
    pallas_call x6, Pallas kernels, call(): pl.pallas_call(kernel, out_shape=[pltpu.VMEM(shape, kind) for shape, kind...  4.03 us
    unnamed x2, local copies, waits for them, and re-layouts  1.31 us
  transfers between devices with their start and end apart: 12, of which 10 were waited for; matrix products, arithmetic and copies ran while one was open for 4% of the time, Pallas kernels for 4%

profile of v4, /device:TPU:0, one launch (start us, length us, event | category | flops | bytes accessed | tf_op | source)
XLA Modules:
  0.0 33.0 jit_solution(12887993030302788889)
XLA Ops:
  0.6 1.0 %shard_map.76.refs_4_.refs_7_.refs_6_ = bf16[1024,128]{1,0:T(8,128)(2,1)S(1)} custom-call(bf16[128,512]{1,0:T(8,128)(2,1)} %query_hbm.1, bf16[128,512]{1,0:T(8,128)(2,1)} %grad_hbm.1), custom_call_target="tpu_custom_call" | custom-call | tf_op jit(solution)/shard_map/pallas_call | solution.py:22
  1.7 0.6 %collective-permute-start.3 = (bf16[1024,128]{1,0:T(8,128)(2,1)S(1)}, bf16[1024,128]{1,0:T(8,128)(2,1)S(1)}, u32[]{:S(2)}, u32[]{:S(2)}) collective-permute-start(bf16[1024,128]{1,0:T(8,128)(2,1)S(1)} %shard_map.76.refs_4_.refs_7_.refs_6_), channel_id=1, source_target_pairs={{0,4},{4,0},{8,12},{12,8},{16,20},{20,16},{24,28},{28,24},{1,5},{5... | collective-permute-start | bytes 786440 | tf_op jit(solution)/shard_map/ppermute | solution.py:180
  2.2 0.8 %shard_map.75.refs_0_ = bf16[128,256]{1,0:T(8,128)(2,1)S(1)} custom-call(bf16[128,128]{1,0:T(8,128)(2,1)} %key_hbm.1, bf16[128,128]{1,0:T(8,128)(2,1)} %value_hbm.1), custom_call_target="tpu_custom_call" | custom-call | tf_op jit(solution)/shard_map/pallas_call | solution.py:22
  3.0 3.5 %collective-permute-start.2 = (bf16[128,256]{1,0:T(8,128)(2,1)S(1)}, bf16[128,256]{1,0:T(8,128)(2,1)S(1)}, u32[]{:S(2)}, u32[]{:S(2)}) collective-permute-start(bf16[128,256]{1,0:T(8,128)(2,1)S(1)} %shard_map.75.refs_0_), channel_id=1, source_target_pairs={{0,24},{4,28},{8,16},{12,20},{16,8},{20,12},{24,0},{28,4},{1,25},{... | collective-permute-start | bytes 196616 | tf_op jit(solution)/shard_map/ppermute | solution.py:180
  6.6 0.5 %collective-permute-start.1 = (bf16[128,256]{1,0:T(8,128)(2,1)S(1)}, bf16[128,256]{1,0:T(8,128)(2,1)S(1)}, u32[]{:S(2)}, u32[]{:S(2)}) collective-permute-start(bf16[128,256]{1,0:T(8,128)(2,1)S(1)} %shard_map.75.refs_0_), channel_id=1, source_target_pairs={{0,16},{4,20},{8,24},{12,28},{16,0},{20,4},{24,8},{28,12},{1,17},{... | collective-permute-start | bytes 196616 | tf_op jit(solution)/shard_map/ppermute | solution.py:180
  7.1 0.1 collective-permute-start
  7.2 2.1 %collective-permute-done.2.refs_3_.refs_2_ = bf16[128,256]{1,0:T(8,128)(2,1)S(1)} collective-permute-done((bf16[128,256]{1,0:T(8,128)(2,1)S(1)}, bf16[128,256]{1,0:T(8,128)(2,1)S(1)}, u32[]{:S(2)}, u32[]{:S(2)}) %collective-permute-start.2) | collective-permute-done | bytes 65568 | tf_op jit(solution)/shard_map/ppermute | solution.py:180
  9.3 1.5 %collective-permute-done.1.refs_2_.refs_1_ = bf16[128,256]{1,0:T(8,128)(2,1)S(1)} collective-permute-done((bf16[128,256]{1,0:T(8,128)(2,1)S(1)}, bf16[128,256]{1,0:T(8,128)(2,1)S(1)}, u32[]{:S(2)}, u32[]{:S(2)}) %collective-permute-start.1) | collective-permute-done | bytes 65568 | tf_op jit(solution)/shard_map/ppermute | solution.py:180
  10.8 0.5 %collective-permute-done.refs_1_.refs_0_ = bf16[128,256]{1,0:T(8,128)(2,1)S(1)} collective-permute-done((bf16[128,256]{1,0:T(8,128)(2,1)S(1)}, bf16[128,256]{1,0:T(8,128)(2,1)S(1)}, u32[]{:S(2)}, u32[]{:S(2)}) %collective-permute-start) | collective-permute-done | bytes 65568 | tf_op jit(solution)/shard_map/ppermute | solution.py:180
  11.3 0.0 collective-permute-done.3.refs_5_.refs_8_.refs_7_
  11.3 0.6 %shard_map.77 = (f32[512,1024]{1,0:T(8,128)S(1)}, bf16[512,1024]{1,0:T(8,128)(2,1)S(1)}, f32[128,1024]{1,0:T(8,128)S(1)}, bf16[128,1024]{1,0:T(8,128)(2,1)S(1)}) custom-call(bf16[128,256]{1,0:T(8,128)(2,1)S(1)} %shard_map.75.refs_0_, bf16[128,256]{1,0:T(8,128)(2,1)S(1)} %collective-permute-done.refs_1_.refs_0_, ...), custom_call_target="tpu_custom_call" | custom-call | tf_op jit(solution)/shard_map/pallas_call | solution.py:22
  11.9 0.1 collective-permute-start.4
  12.0 1.5 %collective-permute-done.4.refs_6_ = bf16[128,1024]{1,0:T(8,128)(2,1)S(1)} collective-permute-done((bf16[128,1024]{1,0:T(8,128)(2,1)S(1)}, bf16[128,1024]{1,0:T(8,128)(2,1)S(1)}, u32[]{:S(2)}, u32[]{:S(2)}) %collective-permute-start.4) | collective-permute-done | bytes 262176 | tf_op jit(solution)/shard_map/ppermute | solution.py:180
  13.6 0.9 %shard_map.78 = (bf16[128,512]{1,0:T(8,128)(2,1)S(1)}, bf16[128,1024]{1,0:T(8,128)(2,1)S(1)}, bf16[384,1024]{1,0:T(8,128)(2,1)S(1)}, bf16[128,256]{1,0:T(8,128)(...) custom-call(bf16[128,256]{1,0:T(8,128)(2,1)S(1)} %collective-permute-done.refs_1_.refs_0_, ...), custom_call_target="tpu_custom_call" | custom-call | tf_op jit(solution)/shard_map/pallas_call | solution.py:22
  14.5 1.2 %collective-permute-start.6 = (bf16[128,256]{1,0:T(8,128)(2,1)S(1)}, bf16[128,256]{1,0:T(8,128)(2,1)S(1)}, u32[]{:S(2)}, u32[]{:S(2)}) collective-permute-start(bf16[128,256]{1,0:T(8,128)(2,1)S(1)} %get-tuple-element.29), channel_id=1, source_target_pairs={{0,8},{4,12},{8,0},{12,4},{16,24},{20,28},{24,16},{28,20},{1,9},{5... | collective-permute-start | bytes 196616 | tf_op jit(solution)/shard_map/ppermute | solution.py:180
  15.7 0.9 %collective-permute-start.7 = (bf16[128,256]{1,0:T(8,128)(2,1)S(1)}, bf16[128,256]{1,0:T(8,128)(2,1)S(1)}, u32[]{:S(2)}, u32[]{:S(2)}) collective-permute-start(bf16[128,256]{1,0:T(8,128)(2,1)S(1)} %get-tuple-element.30), channel_id=1, source_target_pairs={{0,16},{4,20},{8,24},{12,28},{16,0},{20,4},{24,8},{28,12},{1,17},{... | collective-permute-start | bytes 196616 | tf_op jit(solution)/shard_map/ppermute | solution.py:180
  16.6 1.4 %collective-permute-start.8 = (bf16[128,256]{1,0:T(8,128)(2,1)S(1)}, bf16[128,256]{1,0:T(8,128)(2,1)S(1)}, u32[]{:S(2)}, u32[]{:S(2)}) collective-permute-start(bf16[128,256]{1,0:T(8,128)(2,1)S(1)} %get-tuple-element.31), channel_id=1, source_target_pairs={{0,24},{4,28},{8,16},{12,20},{16,8},{20,12},{24,0},{28,4},{1,25},{... | collective-permute-start | bytes 196616 | tf_op jit(solution)/shard_map/ppermute | solution.py:180
  18.0 0.6 %shard_map.79 = (f32[128,256]{1,0:T(8,128)S(1)}, bf16[128,512]{1,0:T(8,128)(2,1)S(1)}, f32[128,512]{1,0:T(8,128)S(1)}, bf16[128,512]{1,0:T(8,128)(2,1)S(1)}) custom-call(bf16[128,256]{1,0:T(8,128)(2,1)S(1)} %shard_map.75.refs_0_, bf16[128,256]{1,0:T(8,128)(2,1)S(1)} %collective-permute-done.refs_1_.refs_0_, ...), custom_call_target="tpu_custom_call" | custom-call | tf_op jit(solution)/shard_map/pallas_call | solution.py:22
  18.6 0.2 collective-permute-done.6
  18.8 1.8 %collective-permute-done.7 = bf16[128,256]{1,0:T(8,128)(2,1)S(1)} collective-permute-done((bf16[128,256]{1,0:T(8,128)(2,1)S(1)}, bf16[128,256]{1,0:T(8,128)(2,1)S(1)}, u32[]{:S(2)}, u32[]{:S(2)}) %collective-permute-start.7) | collective-permute-done | bytes 65568 | tf_op jit(solution)/shard_map/ppermute | solution.py:180
  20.6 1.1 %collective-permute-done.8 = bf16[128,256]{1,0:T(8,128)(2,1)S(1)} collective-permute-done((bf16[128,256]{1,0:T(8,128)(2,1)S(1)}, bf16[128,256]{1,0:T(8,128)(2,1)S(1)}, u32[]{:S(2)}, u32[]{:S(2)}) %collective-permute-start.8) | collective-permute-done | bytes 65568 | tf_op jit(solution)/shard_map/ppermute | solution.py:180
  21.8 3.7 %collective-permute-start.11 = (bf16[128,256]{1,0:T(8,128)(2,1)S(1)}, bf16[128,256]{1,0:T(8,128)(2,1)S(1)}, u32[]{:S(2)}, u32[]{:S(2)}) collective-permute-start(bf16[128,256]{1,0:T(8,128)(2,1)S(1)} %fusion), channel_id=1, source_target_pairs={{0,3},{1,0},{2,1},{3,2},{4,7},{5,4},{6,5},{7,6},{8,11},{9,8},{10,9... | collective-permute-start | bytes 196616 | tf_op jit(solution)/shard_map/ppermute | solution.py:185
  25.5 0.0 collective-permute-start.10
  25.5 1.0 %collective-permute-start.9 = (bf16[128,256]{1,0:T(8,128)(2,1)S(1)}, bf16[128,256]{1,0:T(8,128)(2,1)S(1)}, u32[]{:S(2)}, u32[]{:S(2)}) collective-permute-start(bf16[128,256]{1,0:T(8,128)(2,1)S(1)} %fusion), channel_id=1, source_target_pairs={{0,1},{1,2},{2,3},{3,0},{4,5},{5,6},{6,7},{7,4},{8,9},{9,10},{10,1... | collective-permute-start | bytes 196616 | tf_op jit(solution)/shard_map/ppermute | solution.py:185
  26.5 0.7 %copy.8 = bf16[128,512]{1,0:T(8,128)(2,1)} copy(bf16[128,512]{1,0:T(8,128)(2,1)S(1)} %get-tuple-element.34) | data formatting | bytes 262144
  27.1 0.0 collective-permute-start.5
  27.1 0.2 collective-permute-done.11
  27.4 3.3 %collective-permute-done.10 = bf16[128,256]{1,0:T(8,128)(2,1)S(1)} collective-permute-done((bf16[128,256]{1,0:T(8,128)(2,1)S(1)}, bf16[128,256]{1,0:T(8,128)(2,1)S(1)}, u32[]{:S(2)}, u32[]{:S(2)}) %collective-permute-start.10) | collective-permute-done | bytes 65568 | tf_op jit(solution)/shard_map/ppermute | solution.py:185
  30.6 0.9 %collective-permute-done.9 = bf16[128,256]{1,0:T(8,128)(2,1)S(1)} collective-permute-done((bf16[128,256]{1,0:T(8,128)(2,1)S(1)}, bf16[128,256]{1,0:T(8,128)(2,1)S(1)}, u32[]{:S(2)}, u32[]{:S(2)}) %collective-permute-start.9) | collective-permute-done | bytes 65568 | tf_op jit(solution)/shard_map/ppermute | solution.py:185
  31.5 0.1 add_convert_fusion
  31.6 0.6 %fusion.1 = (bf16[128,128]{1,0:T(8,128)(2,1)}, bf16[128,128]{1,0:T(8,128)(2,1)}) fusion(bf16[128,256]{1,0:T(8,128)(2,1)S(1)} %add_convert_fusion), kind=kLoop, calls=%fused_computation.3 | loop fusion | bytes 131072 | tf_op jit(solution)/shard_map/slice | solution.py:270
  32.2 0.0 collective-permute-done.5.came_ref
  32.2 0.1 shard_map.80
  32.3 0.7 %copy.9 = bf16[128,512]{1,0:T(8,128)(2,1)} copy(bf16[128,512]{1,0:T(8,128)(2,1)S(1)} %shard_map.80) | data formatting | bytes 262144
  (1 shorter events, 0.0 us)
Async XLA Ops:
  1.7 9.6 %collective-permute-start.3 = (bf16[1024,128]{1,0:T(8,128)(2,1)S(1)}, bf16[1024,128]{1,0:T(8,128)(2,1)S(1)}, u32[]{:S(2)}, u32[]{:S(2)}) collective-permute-start(bf16[1024,128]{1,0:T(8,128)(2,1)S(1)} %shard_map.76.refs_4_.refs_7_.refs_6_), channel_id=1, source_target_pairs={{0,4},{4,0},{8,12},{12,8},{16,20},{20,16},{24,28},{28,24},{1,5},{5... | collective-permute-start | bytes 786440 | tf_op jit(solution)/shard_map/ppermute | solution.py:180
  3.0 6.3 %collective-permute-start.2 = (bf16[128,256]{1,0:T(8,128)(2,1)S(1)}, bf16[128,256]{1,0:T(8,128)(2,1)S(1)}, u32[]{:S(2)}, u32[]{:S(2)}) collective-permute-start(bf16[128,256]{1,0:T(8,128)(2,1)S(1)} %shard_map.75.refs_0_), channel_id=1, source_target_pairs={{0,24},{4,28},{8,16},{12,20},{16,8},{20,12},{24,0},{28,4},{1,25},{... | collective-permute-start | bytes 196616 | tf_op jit(solution)/shard_map/ppermute | solution.py:180
  6.6 4.3 %collective-permute-start.1 = (bf16[128,256]{1,0:T(8,128)(2,1)S(1)}, bf16[128,256]{1,0:T(8,128)(2,1)S(1)}, u32[]{:S(2)}, u32[]{:S(2)}) collective-permute-start(bf16[128,256]{1,0:T(8,128)(2,1)S(1)} %shard_map.75.refs_0_), channel_id=1, source_target_pairs={{0,16},{4,20},{8,24},{12,28},{16,0},{20,4},{24,8},{28,12},{1,17},{... | collective-permute-start | bytes 196616 | tf_op jit(solution)/shard_map/ppermute | solution.py:180
  7.1 4.3 %collective-permute-start = (bf16[128,256]{1,0:T(8,128)(2,1)S(1)}, bf16[128,256]{1,0:T(8,128)(2,1)S(1)}, u32[]{:S(2)}, u32[]{:S(2)}) collective-permute-start(bf16[128,256]{1,0:T(8,128)(2,1)S(1)} %shard_map.75.refs_0_), channel_id=1, source_target_pairs={{0,8},{4,12},{8,0},{12,4},{16,24},{20,28},{24,16},{28,20},{1,9},{5... | collective-permute-start | bytes 196616 | tf_op jit(solution)/shard_map/ppermute | solution.py:180
  11.9 1.6 %collective-permute-start.4 = (bf16[128,1024]{1,0:T(8,128)(2,1)S(1)}, bf16[128,1024]{1,0:T(8,128)(2,1)S(1)}, u32[]{:S(2)}, u32[]{:S(2)}) collective-permute-start(bf16[128,1024]{1,0:T(8,128)(2,1)S(1)} %get-tuple-element.21), channel_id=1, source_target_pairs={{0,4},{4,0},{8,12},{12,8},{16,20},{20,16},{24,28},{28,24},{1,5},{5... | collective-permute-start | bytes 786440 | tf_op jit(solution)/shard_map/ppermute | solution.py:180
  14.5 4.3 %collective-permute-start.6 = (bf16[128,256]{1,0:T(8,128)(2,1)S(1)}, bf16[128,256]{1,0:T(8,128)(2,1)S(1)}, u32[]{:S(2)}, u32[]{:S(2)}) collective-permute-start(bf16[128,256]{1,0:T(8,128)(2,1)S(1)} %get-tuple-element.29), channel_id=1, source_target_pairs={{0,8},{4,12},{8,0},{12,4},{16,24},{20,28},{24,16},{28,20},{1,9},{5... | collective-permute-start | bytes 196616 | tf_op jit(solution)/shard_map/ppermute | solution.py:180
  15.7 5.0 %collective-permute-start.7 = (bf16[128,256]{1,0:T(8,128)(2,1)S(1)}, bf16[128,256]{1,0:T(8,128)(2,1)S(1)}, u32[]{:S(2)}, u32[]{:S(2)}) collective-permute-start(bf16[128,256]{1,0:T(8,128)(2,1)S(1)} %get-tuple-element.30), channel_id=1, source_target_pairs={{0,16},{4,20},{8,24},{12,28},{16,0},{20,4},{24,8},{28,12},{1,17},{... | collective-permute-start | bytes 196616 | tf_op jit(solution)/shard_map/ppermute | solution.py:180
  16.6 5.2 %collective-permute-start.8 = (bf16[128,256]{1,0:T(8,128)(2,1)S(1)}, bf16[128,256]{1,0:T(8,128)(2,1)S(1)}, u32[]{:S(2)}, u32[]{:S(2)}) collective-permute-start(bf16[128,256]{1,0:T(8,128)(2,1)S(1)} %get-tuple-element.31), channel_id=1, source_target_pairs={{0,24},{4,28},{8,16},{12,20},{16,8},{20,12},{24,0},{28,4},{1,25},{... | collective-permute-start | bytes 196616 | tf_op jit(solution)/shard_map/ppermute | solution.py:180
  21.8 5.6 %collective-permute-start.11 = (bf16[128,256]{1,0:T(8,128)(2,1)S(1)}, bf16[128,256]{1,0:T(8,128)(2,1)S(1)}, u32[]{:S(2)}, u32[]{:S(2)}) collective-permute-start(bf16[128,256]{1,0:T(8,128)(2,1)S(1)} %fusion), channel_id=1, source_target_pairs={{0,3},{1,0},{2,1},{3,2},{4,7},{5,4},{6,5},{7,6},{8,11},{9,8},{10,9... | collective-permute-start | bytes 196616 | tf_op jit(solution)/shard_map/ppermute | solution.py:185
  25.5 5.2 %collective-permute-start.10 = (bf16[128,256]{1,0:T(8,128)(2,1)S(1)}, bf16[128,256]{1,0:T(8,128)(2,1)S(1)}, u32[]{:S(2)}, u32[]{:S(2)}) collective-permute-start(bf16[128,256]{1,0:T(8,128)(2,1)S(1)} %fusion), channel_id=1, source_target_pairs={{0,2},{1,3},{2,0},{3,1},{4,6},{5,7},{6,4},{7,5},{8,10},{9,11},{10,... | collective-permute-start | bytes 196616 | tf_op jit(solution)/shard_map/ppermute | solution.py:185
  25.5 6.1 %collective-permute-start.9 = (bf16[128,256]{1,0:T(8,128)(2,1)S(1)}, bf16[128,256]{1,0:T(8,128)(2,1)S(1)}, u32[]{:S(2)}, u32[]{:S(2)}) collective-permute-start(bf16[128,256]{1,0:T(8,128)(2,1)S(1)} %fusion), channel_id=1, source_target_pairs={{0,1},{1,2},{2,3},{3,0},{4,5},{5,6},{6,7},{7,4},{8,9},{9,10},{10,1... | collective-permute-start | bytes 196616 | tf_op jit(solution)/shard_map/ppermute | solution.py:185
  27.1 5.1 %collective-permute-start.5 = (bf16[128,512]{1,0:T(8,128)(2,1)S(1)}, bf16[128,512]{1,0:T(8,128)(2,1)S(1)}, u32[]{:S(2)}, u32[]{:S(2)}) collective-permute-start(bf16[128,512]{1,0:T(8,128)(2,1)S(1)} %get-tuple-element.27), channel_id=1, source_target_pairs={{0,4},{4,0},{8,12},{12,8},{16,20},{20,16},{24,28},{28,24},{1,5},{5... | collective-permute-start | bytes 393224 | tf_op jit(solution)/shard_map/ppermute | solution.py:180

commit v5 on v4

--- a/solution.py
+++ b/solution.py
@@ -176,6 +176,22 @@
         out_ref[:, h * head_width : (h + 1) * head_width] = total[:, h * rows : (h + 1) * rows].T
 
 
+def final_kernel(*refs):
+    parts, (key_hbm, value_hbm, key_ref, value_ref, sems) = refs[:-5], refs[-5:]
+    width = key_ref.shape[1]
+    copies = []
+    for i, (target, ref) in enumerate(((key_hbm, key_ref), (value_hbm, value_ref))):
+        columns = slice(i * width, (i + 1) * width)
+        total = parts[0][:, columns]
+        for part in parts[1:]:
+            total = total + part[:, columns].astype(jnp.float32)
+        ref[...] = total.astype(ref.dtype)
+        copies.append(pltpu.make_async_copy(ref, target, sems.at[i]))
+        copies[-1].start()
+    for copy in copies:
+        copy.wait()
+
+
 def partner(array, axis, mask):
     return lax.ppermute(array, axis, [(i, i ^ mask) for i in range(lax.axis_size(axis))])
 
@@ -264,10 +280,18 @@
         query_sum_kernel, [(query_rows.shape, low)], dquery, partner(dquery_other, "seq", 1)
     )
     sent = summed.astype(low)
-    for step in range(1, head_axis):
-        summed = summed + shifted(sent, "head", step).astype(full)
-    summed = summed.astype(low)
-    return (attended, query_grad, summed[:, :head_width], summed[:, head_width:])
+    pieces = [shifted(sent, "head", step) for step in range(1, head_axis)]
+    key_grad, value_grad = pl.pallas_call(
+        final_kernel,
+        out_shape=[jax.ShapeDtypeStruct(x.shape, low) for x in (key_rows, value_rows)],
+        in_specs=[pl.BlockSpec(memory_space=pltpu.VMEM)] * (1 + len(pieces)),
+        out_specs=[pl.BlockSpec(memory_space=pltpu.HBM)] * 2,
+        scratch_shapes=[pltpu.VMEM(x.shape, low) for x in (key_rows, value_rows)]
+        + [pltpu.SemaphoreType.DMA((2,))],
+        compiler_params=pltpu.CompilerParams(vmem_limit_bytes=VMEM_LIMIT),
+        name="final",
+    )(*[pltpu.with_memory_space_constraint(x, pltpu.VMEM) for x in (summed, *pieces)])
+    return (attended, query_grad, key_grad, value_grad)
 
 
 def solution(mesh):

time: 33.2 us -> 33.2 us (level)
  Pallas kernels: 4.03 us -> 4.7 us
  local copies, waits for them, and re-layouts: 1.94 us -> 1.31 us
    pallas_call x0 -> x1, Pallas kernels: none -> 0.66 us  [local(): pl.pallas_call(final_kernel, out_shape=[jax.ShapeDtypeStruct(x.shape, low...]
    slice x1 -> x0, local copies, waits for them, and re-layouts: 0.63 us -> none  [local(): summed[:, head_width:]]
  transfers between devices with their start and end apart: 12 -> 12, of which waited for: 10 -> 10; matrix products, arithmetic and copies ran while one was open for 4% -> 2% of each run, Pallas kernels for 4% -> 6%
where the time goes in v5:
time: 33.2 us; the launch traced here: 33 us
  starting transfers between devices  13.1 us (39%)
  waiting for transfers between devices  13.1 us (39%)
  Pallas kernels  4.7 us (14%)
  local copies, waits for them, and re-layouts  1.31 us (4%)
  between operations  0.72 us (2%)
    ppermute x9, waiting for transfers between devices, partner(): lax.ppermute(array, axis, [(i, i ^ mask) for i in range(lax.axis_size(axi...  8.73 us
    ppermute x9, starting transfers between devices, partner(): lax.ppermute(array, axis, [(i, i ^ mask) for i in range(lax.axis_size(axi...  8.41 us
    ppermute x3, starting transfers between devices, shifted(): lax.ppermute(array, axis, [(i, (i + step) % size) for i in range(size)])  4.67 us
    ppermute x3, waiting for transfers between devices, shifted(): lax.ppermute(array, axis, [(i, (i + step) % size) for i in range(size)])  4.4 us
    pallas_call x6, Pallas kernels, call(): pl.pallas_call(kernel, out_shape=[pltpu.VMEM(shape, kind) for shape, kind...  4.03 us
    unnamed x2, local copies, waits for them, and re-layouts  1.31 us
  transfers between devices with their start and end apart: 12, of which 10 were waited for; matrix products, arithmetic and copies ran while one was open for 2% of the time, Pallas kernels for 6%

profile of v5, /device:TPU:0, one launch (start us, length us, event | category | flops | bytes accessed | tf_op | source)
XLA Modules:
  0.0 33.0 jit_solution(17786783309365364982)
XLA Ops:
  0.6 1.0 %shard_map.76.refs_4_.refs_7_.refs_6_ = bf16[1024,128]{1,0:T(8,128)(2,1)S(1)} custom-call(bf16[128,512]{1,0:T(8,128)(2,1)} %query_hbm.1, bf16[128,512]{1,0:T(8,128)(2,1)} %grad_hbm.1), custom_call_target="tpu_custom_call" | custom-call | tf_op jit(solution)/shard_map/pallas_call | solution.py:22
  1.7 0.6 %collective-permute-start.3 = (bf16[1024,128]{1,0:T(8,128)(2,1)S(1)}, bf16[1024,128]{1,0:T(8,128)(2,1)S(1)}, u32[]{:S(2)}, u32[]{:S(2)}) collective-permute-start(bf16[1024,128]{1,0:T(8,128)(2,1)S(1)} %shard_map.76.refs_4_.refs_7_.refs_6_), channel_id=1, source_target_pairs={{0,4},{4,0},{8,12},{12,8},{16,20},{20,16},{24,28},{28,24},{1,5},{5... | collective-permute-start | bytes 786440 | tf_op jit(solution)/shard_map/ppermute | solution.py:196
  2.2 0.8 %shard_map.75.refs_0_ = bf16[128,256]{1,0:T(8,128)(2,1)S(1)} custom-call(bf16[128,128]{1,0:T(8,128)(2,1)} %key_hbm.1, bf16[128,128]{1,0:T(8,128)(2,1)} %value_hbm.1), custom_call_target="tpu_custom_call" | custom-call | tf_op jit(solution)/shard_map/pallas_call | solution.py:22
  3.0 3.5 %collective-permute-start.2 = (bf16[128,256]{1,0:T(8,128)(2,1)S(1)}, bf16[128,256]{1,0:T(8,128)(2,1)S(1)}, u32[]{:S(2)}, u32[]{:S(2)}) collective-permute-start(bf16[128,256]{1,0:T(8,128)(2,1)S(1)} %shard_map.75.refs_0_), channel_id=1, source_target_pairs={{0,24},{4,28},{8,16},{12,20},{16,8},{20,12},{24,0},{28,4},{1,25},{... | collective-permute-start | bytes 196616 | tf_op jit(solution)/shard_map/ppermute | solution.py:196
  6.6 0.5 %collective-permute-start.1 = (bf16[128,256]{1,0:T(8,128)(2,1)S(1)}, bf16[128,256]{1,0:T(8,128)(2,1)S(1)}, u32[]{:S(2)}, u32[]{:S(2)}) collective-permute-start(bf16[128,256]{1,0:T(8,128)(2,1)S(1)} %shard_map.75.refs_0_), channel_id=1, source_target_pairs={{0,16},{4,20},{8,24},{12,28},{16,0},{20,4},{24,8},{28,12},{1,17},{... | collective-permute-start | bytes 196616 | tf_op jit(solution)/shard_map/ppermute | solution.py:196
  7.1 0.1 collective-permute-start
  7.2 2.1 %collective-permute-done.2.refs_3_.refs_2_ = bf16[128,256]{1,0:T(8,128)(2,1)S(1)} collective-permute-done((bf16[128,256]{1,0:T(8,128)(2,1)S(1)}, bf16[128,256]{1,0:T(8,128)(2,1)S(1)}, u32[]{:S(2)}, u32[]{:S(2)}) %collective-permute-start.2) | collective-permute-done | bytes 65568 | tf_op jit(solution)/shard_map/ppermute | solution.py:196
  9.3 1.5 %collective-permute-done.1.refs_2_.refs_1_ = bf16[128,256]{1,0:T(8,128)(2,1)S(1)} collective-permute-done((bf16[128,256]{1,0:T(8,128)(2,1)S(1)}, bf16[128,256]{1,0:T(8,128)(2,1)S(1)}, u32[]{:S(2)}, u32[]{:S(2)}) %collective-permute-start.1) | collective-permute-done | bytes 65568 | tf_op jit(solution)/shard_map/ppermute | solution.py:196
  10.8 0.5 %collective-permute-done.refs_1_.refs_0_ = bf16[128,256]{1,0:T(8,128)(2,1)S(1)} collective-permute-done((bf16[128,256]{1,0:T(8,128)(2,1)S(1)}, bf16[128,256]{1,0:T(8,128)(2,1)S(1)}, u32[]{:S(2)}, u32[]{:S(2)}) %collective-permute-start) | collective-permute-done | bytes 65568 | tf_op jit(solution)/shard_map/ppermute | solution.py:196
  11.3 0.0 collective-permute-done.3.refs_5_.refs_8_.refs_7_
  11.3 0.6 %shard_map.77 = (f32[512,1024]{1,0:T(8,128)S(1)}, bf16[512,1024]{1,0:T(8,128)(2,1)S(1)}, f32[128,1024]{1,0:T(8,128)S(1)}, bf16[128,1024]{1,0:T(8,128)(2,1)S(1)}) custom-call(bf16[128,256]{1,0:T(8,128)(2,1)S(1)} %shard_map.75.refs_0_, bf16[128,256]{1,0:T(8,128)(2,1)S(1)} %collective-permute-done.refs_1_.refs_0_, ...), custom_call_target="tpu_custom_call" | custom-call | tf_op jit(solution)/shard_map/pallas_call | solution.py:22
  11.9 0.1 collective-permute-start.4
  12.0 1.5 %collective-permute-done.4.refs_6_ = bf16[128,1024]{1,0:T(8,128)(2,1)S(1)} collective-permute-done((bf16[128,1024]{1,0:T(8,128)(2,1)S(1)}, bf16[128,1024]{1,0:T(8,128)(2,1)S(1)}, u32[]{:S(2)}, u32[]{:S(2)}) %collective-permute-start.4) | collective-permute-done | bytes 262176 | tf_op jit(solution)/shard_map/ppermute | solution.py:196
  13.6 0.9 %shard_map.78 = (bf16[128,512]{1,0:T(8,128)(2,1)S(1)}, bf16[128,1024]{1,0:T(8,128)(2,1)S(1)}, bf16[384,1024]{1,0:T(8,128)(2,1)S(1)}, bf16[128,256]{1,0:T(8,128)(...) custom-call(bf16[128,256]{1,0:T(8,128)(2,1)S(1)} %collective-permute-done.refs_1_.refs_0_, ...), custom_call_target="tpu_custom_call" | custom-call | tf_op jit(solution)/shard_map/pallas_call | solution.py:22
  14.5 1.2 %collective-permute-start.6 = (bf16[128,256]{1,0:T(8,128)(2,1)S(1)}, bf16[128,256]{1,0:T(8,128)(2,1)S(1)}, u32[]{:S(2)}, u32[]{:S(2)}) collective-permute-start(bf16[128,256]{1,0:T(8,128)(2,1)S(1)} %get-tuple-element.31), channel_id=1, source_target_pairs={{0,8},{4,12},{8,0},{12,4},{16,24},{20,28},{24,16},{28,20},{1,9},{5... | collective-permute-start | bytes 196616 | tf_op jit(solution)/shard_map/ppermute | solution.py:196
  15.7 0.9 %collective-permute-start.7 = (bf16[128,256]{1,0:T(8,128)(2,1)S(1)}, bf16[128,256]{1,0:T(8,128)(2,1)S(1)}, u32[]{:S(2)}, u32[]{:S(2)}) collective-permute-start(bf16[128,256]{1,0:T(8,128)(2,1)S(1)} %get-tuple-element.32), channel_id=1, source_target_pairs={{0,16},{4,20},{8,24},{12,28},{16,0},{20,4},{24,8},{28,12},{1,17},{... | collective-permute-start | bytes 196616 | tf_op jit(solution)/shard_map/ppermute | solution.py:196
  16.6 1.4 %collective-permute-start.8 = (bf16[128,256]{1,0:T(8,128)(2,1)S(1)}, bf16[128,256]{1,0:T(8,128)(2,1)S(1)}, u32[]{:S(2)}, u32[]{:S(2)}) collective-permute-start(bf16[128,256]{1,0:T(8,128)(2,1)S(1)} %get-tuple-element.33), channel_id=1, source_target_pairs={{0,24},{4,28},{8,16},{12,20},{16,8},{20,12},{24,0},{28,4},{1,25},{... | collective-permute-start | bytes 196616 | tf_op jit(solution)/shard_map/ppermute | solution.py:196
  18.0 0.6 %shard_map.79 = (f32[128,256]{1,0:T(8,128)S(1)}, bf16[128,512]{1,0:T(8,128)(2,1)S(1)}, f32[128,512]{1,0:T(8,128)S(1)}, bf16[128,512]{1,0:T(8,128)(2,1)S(1)}) custom-call(bf16[128,256]{1,0:T(8,128)(2,1)S(1)} %shard_map.75.refs_0_, bf16[128,256]{1,0:T(8,128)(2,1)S(1)} %collective-permute-done.refs_1_.refs_0_, ...), custom_call_target="tpu_custom_call" | custom-call | tf_op jit(solution)/shard_map/pallas_call | solution.py:22
  18.6 0.1 collective-permute-start.5
  18.7 0.1 collective-permute-done.6
  18.8 1.8 %collective-permute-done.7 = bf16[128,256]{1,0:T(8,128)(2,1)S(1)} collective-permute-done((bf16[128,256]{1,0:T(8,128)(2,1)S(1)}, bf16[128,256]{1,0:T(8,128)(2,1)S(1)}, u32[]{:S(2)}, u32[]{:S(2)}) %collective-permute-start.7) | collective-permute-done | bytes 65568 | tf_op jit(solution)/shard_map/ppermute | solution.py:196
  20.6 1.1 %collective-permute-done.8 = bf16[128,256]{1,0:T(8,128)(2,1)S(1)} collective-permute-done((bf16[128,256]{1,0:T(8,128)(2,1)S(1)}, bf16[128,256]{1,0:T(8,128)(2,1)S(1)}, u32[]{:S(2)}, u32[]{:S(2)}) %collective-permute-start.8) | collective-permute-done | bytes 65568 | tf_op jit(solution)/shard_map/ppermute | solution.py:196
  21.8 3.7 %collective-permute-start.11 = (bf16[128,256]{1,0:T(8,128)(2,1)S(1)}, bf16[128,256]{1,0:T(8,128)(2,1)S(1)}, u32[]{:S(2)}, u32[]{:S(2)}) collective-permute-start(bf16[128,256]{1,0:T(8,128)(2,1)S(1)} %get-tuple-element.36), channel_id=1, source_target_pairs={{0,3},{1,0},{2,1},{3,2},{4,7},{5,4},{6,5},{7,6},{8,11},{9,8},{10,9... | collective-permute-start | bytes 196616 | tf_op jit(solution)/shard_map/ppermute | solution.py:201
  25.5 0.0 collective-permute-start.10
  25.5 1.0 %collective-permute-start.9 = (bf16[128,256]{1,0:T(8,128)(2,1)S(1)}, bf16[128,256]{1,0:T(8,128)(2,1)S(1)}, u32[]{:S(2)}, u32[]{:S(2)}) collective-permute-start(bf16[128,256]{1,0:T(8,128)(2,1)S(1)} %get-tuple-element.36), channel_id=1, source_target_pairs={{0,1},{1,2},{2,3},{3,0},{4,5},{5,6},{6,7},{7,4},{8,9},{9,10},{10,1... | collective-permute-start | bytes 196616 | tf_op jit(solution)/shard_map/ppermute | solution.py:201
  26.5 0.7 %copy.8 = bf16[128,512]{1,0:T(8,128)(2,1)} copy(bf16[128,512]{1,0:T(8,128)(2,1)S(1)} %get-tuple-element.38) | data formatting | bytes 262144
  27.1 0.2 collective-permute-done.11.refs_3_
  27.4 3.3 %collective-permute-done.10.refs_2_ = bf16[128,256]{1,0:T(8,128)(2,1)S(1)} collective-permute-done((bf16[128,256]{1,0:T(8,128)(2,1)S(1)}, bf16[128,256]{1,0:T(8,128)(2,1)S(1)}, u32[]{:S(2)}, u32[]{:S(2)}) %collective-permute-start.10) | collective-permute-done | bytes 65568 | tf_op jit(solution)/shard_map/ppermute | solution.py:201
  30.6 0.9 %collective-permute-done.9.refs_1_ = bf16[128,256]{1,0:T(8,128)(2,1)S(1)} collective-permute-done((bf16[128,256]{1,0:T(8,128)(2,1)S(1)}, bf16[128,256]{1,0:T(8,128)(2,1)S(1)}, u32[]{:S(2)}, u32[]{:S(2)}) %collective-permute-start.9) | collective-permute-done | bytes 65568 | tf_op jit(solution)/shard_map/ppermute | solution.py:201
  31.5 0.7 %final.1 = (bf16[128,128]{1,0:T(8,128)(2,1)}, bf16[128,128]{1,0:T(8,128)(2,1)}) custom-call(f32[128,256]{1,0:T(8,128)S(1)} %get-tuple-element.37.refs_0_, bf16[128,256]{1,0:T(8,128)(2,1)S(1)} %collective-permute-done.9.refs_1_, bf16[128,256]{1,0:T(8,128)(2,1)S(1)} %collective-permute-done.10.refs_2_, bf16[128,256]{1,0:T(8,128)(2,1)S(1)} %collective-permute-done.11.refs_3_), custom_call_target="tpu_custom_call" | custom-call | tf_op jit(solution)/shard_map/final/pallas_call | solution.py:284
  32.2 0.0 collective-permute-done.5.came_ref
  32.2 0.1 shard_map.80
  32.3 0.7 %copy.9 = bf16[128,512]{1,0:T(8,128)(2,1)} copy(bf16[128,512]{1,0:T(8,128)(2,1)S(1)} %shard_map.80) | data formatting | bytes 262144
  (1 shorter events, 0.0 us)
Async XLA Ops:
  1.7 9.6 %collective-permute-start.3 = (bf16[1024,128]{1,0:T(8,128)(2,1)S(1)}, bf16[1024,128]{1,0:T(8,128)(2,1)S(1)}, u32[]{:S(2)}, u32[]{:S(2)}) collective-permute-start(bf16[1024,128]{1,0:T(8,128)(2,1)S(1)} %shard_map.76.refs_4_.refs_7_.refs_6_), channel_id=1, source_target_pairs={{0,4},{4,0},{8,12},{12,8},{16,20},{20,16},{24,28},{28,24},{1,5},{5... | collective-permute-start | bytes 786440 | tf_op jit(solution)/shard_map/ppermute | solution.py:196
  3.0 6.3 %collective-permute-start.2 = (bf16[128,256]{1,0:T(8,128)(2,1)S(1)}, bf16[128,256]{1,0:T(8,128)(2,1)S(1)}, u32[]{:S(2)}, u32[]{:S(2)}) collective-permute-start(bf16[128,256]{1,0:T(8,128)(2,1)S(1)} %shard_map.75.refs_0_), channel_id=1, source_target_pairs={{0,24},{4,28},{8,16},{12,20},{16,8},{20,12},{24,0},{28,4},{1,25},{... | collective-permute-start | bytes 196616 | tf_op jit(solution)/shard_map/ppermute | solution.py:196
  6.6 4.3 %collective-permute-start.1 = (bf16[128,256]{1,0:T(8,128)(2,1)S(1)}, bf16[128,256]{1,0:T(8,128)(2,1)S(1)}, u32[]{:S(2)}, u32[]{:S(2)}) collective-permute-start(bf16[128,256]{1,0:T(8,128)(2,1)S(1)} %shard_map.75.refs_0_), channel_id=1, source_target_pairs={{0,16},{4,20},{8,24},{12,28},{16,0},{20,4},{24,8},{28,12},{1,17},{... | collective-permute-start | bytes 196616 | tf_op jit(solution)/shard_map/ppermute | solution.py:196
  7.1 4.3 %collective-permute-start = (bf16[128,256]{1,0:T(8,128)(2,1)S(1)}, bf16[128,256]{1,0:T(8,128)(2,1)S(1)}, u32[]{:S(2)}, u32[]{:S(2)}) collective-permute-start(bf16[128,256]{1,0:T(8,128)(2,1)S(1)} %shard_map.75.refs_0_), channel_id=1, source_target_pairs={{0,8},{4,12},{8,0},{12,4},{16,24},{20,28},{24,16},{28,20},{1,9},{5... | collective-permute-start | bytes 196616 | tf_op jit(solution)/shard_map/ppermute | solution.py:196
  11.9 1.6 %collective-permute-start.4 = (bf16[128,1024]{1,0:T(8,128)(2,1)S(1)}, bf16[128,1024]{1,0:T(8,128)(2,1)S(1)}, u32[]{:S(2)}, u32[]{:S(2)}) collective-permute-start(bf16[128,1024]{1,0:T(8,128)(2,1)S(1)} %get-tuple-element.23), channel_id=1, source_target_pairs={{0,4},{4,0},{8,12},{12,8},{16,20},{20,16},{24,28},{28,24},{1,5},{5... | collective-permute-start | bytes 786440 | tf_op jit(solution)/shard_map/ppermute | solution.py:196
  14.5 4.3 %collective-permute-start.6 = (bf16[128,256]{1,0:T(8,128)(2,1)S(1)}, bf16[128,256]{1,0:T(8,128)(2,1)S(1)}, u32[]{:S(2)}, u32[]{:S(2)}) collective-permute-start(bf16[128,256]{1,0:T(8,128)(2,1)S(1)} %get-tuple-element.31), channel_id=1, source_target_pairs={{0,8},{4,12},{8,0},{12,4},{16,24},{20,28},{24,16},{28,20},{1,9},{5... | collective-permute-start | bytes 196616 | tf_op jit(solution)/shard_map/ppermute | solution.py:196
  15.7 5.0 %collective-permute-start.7 = (bf16[128,256]{1,0:T(8,128)(2,1)S(1)}, bf16[128,256]{1,0:T(8,128)(2,1)S(1)}, u32[]{:S(2)}, u32[]{:S(2)}) collective-permute-start(bf16[128,256]{1,0:T(8,128)(2,1)S(1)} %get-tuple-element.32), channel_id=1, source_target_pairs={{0,16},{4,20},{8,24},{12,28},{16,0},{20,4},{24,8},{28,12},{1,17},{... | collective-permute-start | bytes 196616 | tf_op jit(solution)/shard_map/ppermute | solution.py:196
  16.6 5.2 %collective-permute-start.8 = (bf16[128,256]{1,0:T(8,128)(2,1)S(1)}, bf16[128,256]{1,0:T(8,128)(2,1)S(1)}, u32[]{:S(2)}, u32[]{:S(2)}) collective-permute-start(bf16[128,256]{1,0:T(8,128)(2,1)S(1)} %get-tuple-element.33), channel_id=1, source_target_pairs={{0,24},{4,28},{8,16},{12,20},{16,8},{20,12},{24,0},{28,4},{1,25},{... | collective-permute-start | bytes 196616 | tf_op jit(solution)/shard_map/ppermute | solution.py:196
  18.6 13.6 %collective-permute-start.5 = (bf16[128,512]{1,0:T(8,128)(2,1)S(1)}, bf16[128,512]{1,0:T(8,128)(2,1)S(1)}, u32[]{:S(2)}, u32[]{:S(2)}) collective-permute-start(bf16[128,512]{1,0:T(8,128)(2,1)S(1)} %get-tuple-element.29), channel_id=1, source_target_pairs={{0,4},{4,0},{8,12},{12,8},{16,20},{20,16},{24,28},{28,24},{1,5},{5... | collective-permute-start | bytes 393224 | tf_op jit(solution)/shard_map/ppermute | solution.py:196
  21.8 5.6 %collective-permute-start.11 = (bf16[128,256]{1,0:T(8,128)(2,1)S(1)}, bf16[128,256]{1,0:T(8,128)(2,1)S(1)}, u32[]{:S(2)}, u32[]{:S(2)}) collective-permute-start(bf16[128,256]{1,0:T(8,128)(2,1)S(1)} %get-tuple-element.36), channel_id=1, source_target_pairs={{0,3},{1,0},{2,1},{3,2},{4,7},{5,4},{6,5},{7,6},{8,11},{9,8},{10,9... | collective-permute-start | bytes 196616 | tf_op jit(solution)/shard_map/ppermute | solution.py:201
  25.5 5.2 %collective-permute-start.10 = (bf16[128,256]{1,0:T(8,128)(2,1)S(1)}, bf16[128,256]{1,0:T(8,128)(2,1)S(1)}, u32[]{:S(2)}, u32[]{:S(2)}) collective-permute-start(bf16[128,256]{1,0:T(8,128)(2,1)S(1)} %get-tuple-element.36), channel_id=1, source_target_pairs={{0,2},{1,3},{2,0},{3,1},{4,6},{5,7},{6,4},{7,5},{8,10},{9,11},{10,... | collective-permute-start | bytes 196616 | tf_op jit(solution)/shard_map/ppermute | solution.py:201
  25.5 6.1 %collective-permute-start.9 = (bf16[128,256]{1,0:T(8,128)(2,1)S(1)}, bf16[128,256]{1,0:T(8,128)(2,1)S(1)}, u32[]{:S(2)}, u32[]{:S(2)}) collective-permute-start(bf16[128,256]{1,0:T(8,128)(2,1)S(1)} %get-tuple-element.36), channel_id=1, source_target_pairs={{0,1},{1,2},{2,3},{3,0},{4,5},{5,6},{6,7},{7,4},{8,9},{9,10},{10,1... | collective-permute-start | bytes 196616 | tf_op jit(solution)/shard_map/ppermute | solution.py:201
